TPU v7x, 256 devices: a whole 4x4x8 slice. The times are simulated.
256 devices in a mesh: dom: 64 (over x_lo, z, y), orb: 4 (over x_hi, core).
Axes of the slice: x: 4 (x_hi: 2, x_lo: 2; x = x_hi * 2 + x_lo), y: 4, z: 8, core: 2. Of those that a mesh axis runs over, the one named last changes fastest.
Arguments:
- orbitals: bfloat16 [128, 4, 1024, 512], P('dom', None, None, 'orb'), may hold values from -6 to 6
- slot_ids: int32 [128, 4], P('dom'), may hold values from 0 to 15, as said below
- slot_count: int32 [128], P('dom'), may hold values from 1 to 4, as said below
- band_tiles: bfloat16 [16, 3, 512, 512], P(None, None, 'dom', 'orb'), may hold values from -0.15625 to 0.15625
- pattern: int32 [16, 3], replicated, may hold values 0 or 1
- occupation: float32 [16, 512], P(None, 'orb'), may hold values from 0.0005 to 0.005
Outputs:
- rotated: bfloat16 [128, 4, 1024, 512], P('dom', None, None, 'orb')
- density: float32 [128, 1024], P('dom')
Inputs may be any that keep to these rules, and one draw needn't show every extreme that they name: `slot_ids`: each row names 4 consecutive orbital blocks counted modulo 16: slot l holds (s + l) mod 16, where the first block s of a grid block may be any of the 16 blocks. The slots in use on grid block g are its first slot_count[g]; some grid block uses all 4.
All inputs are finite; a program needn't handle non-finite values.
Results may differ from a plain program's by a relative error of at most 0.00094.
Values may be sent and summed in bfloat16 or wider, within the bound.
No kernel may reach another device: no remote copies, remote signals or barrier semaphores. Data moves between devices by JAX's collectives and lax.ppermute only.
A program may use at most 128 MiB of HBM per device.

v0:
```python
import jax
import jax.numpy as jnp
from jax import lax
from jax.sharding import Mesh
from jax.sharding import PartitionSpec as P

DOM = ("dom_0", "dom_1", "dom_2")


def laid_out(tiles, dim):
    shape = list(tiles.shape[1:])
    shape[dim] *= tiles.shape[0]
    return jnp.moveaxis(tiles, 0, dim).reshape(shape)


def all_blocks(x, axes, sequence):
    tiles = x
    for k in sequence:
        tiles = lax.all_gather(tiles, axes[k])
    done = sequence[::-1]
    back = [done.index(k) for k in range(len(axes))]
    tiles = tiles.transpose(*back, *range(len(axes), tiles.ndim))
    return tiles.reshape(-1, *x.shape)


def whole_of(x, axes, sequence, dim):
    return laid_out(all_blocks(x, axes, sequence), dim)


def from_everyone(x, axis):
    peers = lax.axis_size(axis)
    return lax.all_to_all(jnp.broadcast_to(x[None], (peers, *x.shape)), axis, 0, 0, tiled=True)


def of_everyone(x, axis):
    return from_everyone(x, axis).sum(axis=0)


def select_tiles(band_full, pattern, slot_ids, slot_count):
    slots_per = slot_ids.shape[1]
    band_count = pattern.shape[1]
    half_band = (band_count - 1) // 2
    active = jnp.arange(slots_per, dtype=jnp.int32)[None, :] < slot_count[:, None]
    source = slot_ids[:, :, None]
    target = slot_ids[:, None, :]
    offset = target - source + half_band
    inside = (offset >= 0) & (offset < band_count)
    column = jnp.clip(offset, 0, band_count - 1)
    keeping = inside & (pattern[source, column] == 1) & active[:, :, None] & active[:, None, :]
    picked = band_full[source, column]
    return jnp.where(keeping[:, :, :, None, None], picked, jnp.zeros((), picked.dtype))


def rotate(values, tile_set):
    return jnp.einsum("glpi,glmij->gmpj", values, tile_set, preferred_element_type=jnp.float32)


def local(orbitals, slot_ids, slot_count, band_tiles, pattern, occupation):
    all_rows = whole_of(band_tiles, DOM, (0, 1, 2), 2)
    tile_set = select_tiles(all_rows, pattern, slot_ids, slot_count)
    rotated_f = rotate(lax.all_gather(orbitals, "orb", axis=3, tiled=True), tile_set)
    rotated = rotated_f.astype(jnp.bfloat16)
    onehot = (
        slot_ids[:, :, None] == jnp.arange(occupation.shape[0], dtype=jnp.int32)[None, None, :]
    ).astype(jnp.float32)
    weights = jnp.einsum("glb,bj->glj", onehot, occupation, precision=lax.Precision.HIGHEST)
    widened = rotated.astype(jnp.float32)
    square = widened * widened
    partial_density = jnp.einsum("gmpj,gmj->gp", square, weights, precision=lax.Precision.HIGHEST)
    density = of_everyone(partial_density, "orb")
    return (rotated, density)


def solution(mesh):
    torus = Mesh(
        mesh.devices.reshape(2, 8, 4, mesh.shape["orb"]), ("dom_0", "dom_1", "dom_2", "orb")
    )
    return jax.shard_map(
        local,
        mesh=torus,
        in_specs=(
            P(DOM, None, None, "orb"),
            P(DOM, None),
            P(DOM),
            P(None, None, DOM, "orb"),
            P(),
            P(None, "orb"),
        ),
        out_specs=(P(DOM, None, None, "orb"), P(DOM, None)),
        check_vma=False,
    )
```

profile of v0, /device:TPU:1, one launch (start us, length us, event | category | flops | bytes accessed | tf_op | source)
XLA Modules:
  0.0 223.0 jit_solution(2459626745871815533)
XLA Ops:
  7.2 0.0 copy-start
  7.2 0.0 copy-start.2
  7.2 0.0 copy-start.1
  7.2 0.0 copy-start.3
  7.2 0.0 all-gather.9.cloned.1.call-start
  7.3 6.5 %all-gather = bf16[32,3,8,128]{3,2,1,0:T(8,128)(2,1)} all-gather(bf16[16,3,8,128]{3,2,1,0:T(8,128)(2,1)} %param.9), channel_id=2, replica_groups=mesh['dom_0'=2,'dom_1'=8,'dom_2'=4,'orb'=4] {'dom_0'}, dimensions={0}, use_global_device_ids=true | all-gather | bytes 294912 | tf_op jit(solution)/shard_map/all_gather | solution.py:19
  13.7 0.0 all-gather.9.cloned.1.call-update
  13.8 0.0 all-gather.11.cloned.1.call-start
  13.8 39.6 %all-gather.9.cloned.1.call-done = bf16[16,16,3,8,128]{4,3,2,1,0:T(8,128)(2,1)} async-done(((bf16[2,16,3,8,128]{4,3,2,1,0:T(8,128)(2,1)}), bf16[16,16,3,8,128]{4,3,2,1,0:T(8,128)(2,1)}) %all-gather.9.cloned.1.call-update) | async-done | bytes 1572880 | tf_op jit(solution)/shard_map/all_gather | solution.py:19
  53.4 0.0 all-gather.11.cloned.1.call-update
  53.4 0.0 all-gather.7.cloned.1.call-start
  53.5 0.7 all-gather.7.cloned.1.call-update
  54.2 0.7 fusion.26
  54.8 0.8 fusion.17
  55.7 0.1 reshape.85
  55.8 0.0 copy-done.1
  55.8 0.8 gather_fusion
  56.5 0.1 reshape.101
  56.6 0.0 copy-done.3
  56.6 0.1 iota_compare_fusion.2
  56.7 0.0 copy-done.2
  56.7 0.1 fusion.23
  56.8 0.0 copy-done
  56.8 0.2 fusion.13
  57.0 68.7 %all-gather.11.cloned.1.call-done = bf16[32,2,16,3,8,128]{5,4,3,2,1,0:T(8,128)(2,1)} async-done(((bf16[8,2,16,3,8,128]{5,4,3,2,1,0:T(8,128)(2,1)}), bf16[32,2,16,3,8,128]{5,4,3,2,1,0:T(8,128)(2,1)}) %all-gather.11.cloned.1.call-update) | async-done | bytes 6291472 | tf_op jit(solution)/shard_map/all_gather | solution.py:19
  125.7 3.9 %copy.25 = bf16[2,8,4,16,3,8,128]{6,5,4,3,2,1,0:T(8,128)(2,1)S(1)} copy(bf16[2,8,4,16,3,8,128]{6,5,4,3,0,1,2:T(8,128)(2,1)} %bitcast.43) | data formatting | bytes 12582912 | tf_op jit(solution)/shard_map/transpose | solution.py:22
  129.6 4.9 %copy_bitcast_fusion = bf16[16,3,512,128]{3,2,1,0:T(8,128)(2,1)} fusion(bf16[2,8,4,16,3,8,128]{6,5,4,3,2,1,0:T(8,128)(2,1)S(1)} %copy.25), kind=kLoop, calls=%fused_computation.4 | loop fusion | bytes 12582912 | tf_op jit(solution)/shard_map/reshape | solution.py:13
  134.5 5.8 %gather_fusion.1 = bf16[32,512,128]{2,1,0:T(8,128)(2,1)} fusion(bf16[16,3,512,128]{3,2,1,0:T(8,128)(2,1)} %copy_bitcast_fusion, s32[32]{0:T(128)S(1)} %reshape.85), kind=kCustom, calls=%fused_computation.1 | custom fusion | bytes 8388864 | tf_op jit(solution)/shard_map/gather | solution.py:50
  140.3 54.4 %all-gather.7.cloned.1.call-done = bf16[2,4,1024,512]{3,2,1,0:T(8,128)(2,1)} async-done(((bf16[2,4,1024,128]{3,2,1,0:T(8,128)(2,1)}), bf16[2,4,1024,512]{3,2,1,0:T(8,128)(2,1)}) %all-gather.7.cloned.1.call-update) | async-done | bytes 8388624 | tf_op jit(solution)/shard_map/all_gather | solution.py:61
  194.7 9.8 %fusion.7 = bf16[2,4,1024,128]{2,3,1,0:T(8,128)(2,1)S(1)} fusion(bf16[2,4,1024,512]{3,2,1,0:T(8,128)(2,1)} %all-gather.7.cloned.1.call-done, bf16[2,4,4,512,128]{4,3,2,1,0:T(8,128)(2,1)} %bitcast.44, pred[2,4,4]{2,1,0:T(4,128)(4,1)S(1)} %fusion.23), kind=kOutput, calls=%fused_computation.11 | convolution fusion | flops 4298113024 | bytes 14680096 | tf_op jit(solution)/shard_map/glpi,glmij->gmpj/dot_general | solution.py:55
  204.6 2.5 %fusion.2 = f32[2,1,1024,1]{2,1,3,0:T(1,128)S(1)} fusion(f32[2,4,128,1]{2,3,1,0:T(1,128)S(1)} %bitcast.48, bf16[2,4,1024,128]{2,3,1,0:T(8,128)(2,1)S(1)} %fusion.7), kind=kOutput, calls=%fused_computation.6 | convolution fusion | flops 14680064 | bytes 2109440 | tf_op jit(solution)/shard_map/gmpj,gmj->gp/dot_general | solution.py:69
  207.1 0.6 broadcast_in_dim.15
  207.7 3.5 %all-to-all-start = ((f32[4,2,1024]{2,1,0:T(2,128)}), f32[4,2,1024]{2,1,0:T(2,128)S(1)}, u32[]{:S(2)}, u32[]{:S(2)}) async-start(f32[4,2,1024]{2,1,0:T(2,128)} %broadcast_in_dim.15), calls=%async_computation | async-start | bytes 65536 | tf_op jit(solution)/shard_map/all_to_all | solution.py:32
  211.2 2.5 %copy.29 = bf16[2,4,1024,128]{3,2,1,0:T(8,128)(2,1)} copy(bf16[2,4,1024,128]{2,3,1,0:T(8,128)(2,1)S(1)} %fusion.7) | data formatting | bytes 4194304
  213.7 2.1 all-to-all-done
  215.9 0.6 reduce_sum.9
  (2 shorter events, 0.0 us)
Async XLA Ops:
  7.2 49.6 %copy-start = (f32[16,128]{1,0:T(8,128)S(1)}, f32[16,128]{1,0:T(8,128)}, u32[]{:S(2)}) copy-start(f32[16,128]{1,0:T(8,128)} %param.11) | copy-start | bytes 24580
  7.2 49.5 %copy-start.2 = (s32[2,4]{1,0:T(2,128)S(1)}, s32[2,4]{1,0:T(2,128)}, u32[]{:S(2)}) copy-start(s32[2,4]{1,0:T(2,128)} %param.7) | copy-start | bytes 100
  7.2 48.6 %copy-start.1 = (s32[16,3]{0,1:T(4,128)S(1)}, s32[16,3]{0,1:T(4,128)}, u32[]{:S(2)}) copy-start(s32[16,3]{0,1:T(4,128)} %param.10) | copy-start | bytes 580
  7.2 49.4 %copy-start.3 = (s32[2]{0:T(128)S(1)}, s32[2]{0:T(128)}, u32[]{:S(2)}) copy-start(s32[2]{0:T(128)} %param.8) | copy-start | bytes 28
  7.2 46.2 %all-gather.9.cloned.1.call-start = ((), (), s32[]{:S(2)}) async-start(), calls=%async_computation.2 | async-start | bytes 1769472 | tf_op jit(solution)/shard_map/all_gather | solution.py:19
  13.8 111.9 %all-gather.11.cloned.1.call-start = ((), (), s32[]{:S(2)}) async-start(), calls=%async_computation.3 | async-start | bytes 7864320 | tf_op jit(solution)/shard_map/all_gather | solution.py:19
  53.4 141.3 %all-gather.7.cloned.1.call-start = ((), (), s32[]{:S(2)}) async-start(), calls=%async_computation.1 | async-start | bytes 10485760 | tf_op jit(solution)/shard_map/all_gather | solution.py:61
  207.7 8.2 %all-to-all-start = ((f32[4,2,1024]{2,1,0:T(2,128)}), f32[4,2,1024]{2,1,0:T(2,128)S(1)}, u32[]{:S(2)}, u32[]{:S(2)}) async-start(f32[4,2,1024]{2,1,0:T(2,128)} %broadcast_in_dim.15), calls=%async_computation | async-start | bytes 65536 | tf_op jit(solution)/shard_map/all_to_all | solution.py:32
Sparse Core Ops, SparseCore 0:
  13.9 39.4 all-gather.8
  55.2 70.4 all-gather.10
  127.5 67.1 all-gather.6
where the time goes:
time: 223 us
  waiting for transfers between devices  166 us (74%)
  local copies, waits for them, and re-layouts  18.7 us (8%)
  between operations  13.8 us (6%)
  matrix products  12.5 us (6%)
  blocking collectives  6.49 us (3%)
  starting transfers between devices  3.61 us (2%)
  other arithmetic  2.3 us (1%)
    all_gather x2, waiting for transfers between devices, all_blocks(): tiles = lax.all_gather(tiles, axes[k])  108 us
    all_gather x1, waiting for transfers between devices, local(): lax.all_gather(orbitals, 'orb', axis=3, tiled=True)  54.4 us
    dot_general x1, matrix products, rotate(): jnp.einsum('glpi,glmij->gmpj', values, tile_set, preferred_element_type=j...  9.84 us
    all_gather x1, blocking collectives, all_blocks(): tiles = lax.all_gather(tiles, axes[k])  6.49 us
    gather x1, local copies, waits for them, and re-layouts, select_tiles(): picked = band_full[source, column]  5.83 us
    reshape x1, local copies, waits for them, and re-layouts, laid_out(): return jnp.moveaxis(tiles, 0, dim).reshape(shape)  4.87 us
  transfers between devices with their start and end apart: 4, of which 4 were waited for; matrix products, arithmetic and copies ran while one was open for 9% of the time, Pallas kernels for 0%

commit v1 on v0

v1 whole, which is shorter than its diff:
```python
import jax
import jax.numpy as jnp
from jax import lax
from jax.experimental import pallas as pl
from jax.experimental.pallas import tpu as pltpu
from jax.sharding import Mesh
from jax.sharding import PartitionSpec as P


DOM = ("xl", "z", "y")
ORB = ("xh", "c")

NEAR = (1, 3, 7, 2)
FAR = (6, 5, 4)
PEERS = (1, 3, 2)
PAIRS = tuple((l, l) for l in range(4)) + tuple((l, l + 1) for l in range(3)) + tuple((l + 1, l) for l in range(3))
CHUNK = 256


def swap(x, axis, distance=1):
    size = lax.axis_size(axis)
    return lax.ppermute(x, axis, [(i, i ^ distance) for i in range(size)])


def pack_kernel(*refs):
    peers = len(PEERS)
    ids, pieces, outs = refs[:peers], refs[peers:-peers], refs[-peers:]
    for g in range(2):
        for n, (source, target) in enumerate(PAIRS):
            for slots, out in zip(ids, outs):
                tile = slots[g, source] * 3 + (target - source + 1)
                for k, piece in enumerate(pieces):
                    for half in range(2):
                        out[g * len(PAIRS) + n, k, half] = piece[half, tile]


def pack(slots, pieces):
    shape = jax.ShapeDtypeStruct((2 * len(PAIRS), len(pieces), *pieces[0].shape[:1], *pieces[0].shape[2:]), pieces[0].dtype)
    smem = pl.BlockSpec(memory_space=pltpu.SMEM)
    vmem = pl.BlockSpec(memory_space=pltpu.VMEM)
    return pl.pallas_call(
        pack_kernel,
        out_shape=[shape] * len(slots),
        in_specs=[smem] * len(slots) + [vmem] * len(pieces),
        out_specs=[vmem] * len(slots),
        cost_estimate=pl.CostEstimate(flops=1000000, bytes_accessed=2000000, transcendentals=0),
    )(*slots, *pieces)


def rotate_kernel(meta, slots, counts, pattern, *refs):
    own = refs[: 1 + len(NEAR) + len(FAR)]
    rest = refs[len(own) :]
    first, rest = rest[: len(PEERS)], rest[len(PEERS) :]
    second, rest = rest[: len(PEERS)], rest[len(PEERS) :]
    occupation, quarters, (out, density), (weights,) = rest[0], rest[1:5], rest[5:7], rest[7:]
    g = pl.program_id(0)
    my_xl, my_z, my_y, my_q = meta[0], meta[1], meta[2], meta[3]
    distances = (0,) + NEAR + FAR
    pairs = len(PAIRS)

    @pl.when(pl.program_id(1) == 0)
    def _():
        zero = jnp.zeros((8, 128), weights.dtype)
        weights[0, 2, :, :, :, :, :128] = jnp.zeros((4, 4, 4, 8, 128), weights.dtype)
        weights[1, 0, :, :, :, :, 128:] = jnp.zeros((4, 4, 4, 8, 128), weights.dtype)
        for n, (source, target) in enumerate(PAIRS):
            s, t = slots[g, source], slots[g, target]
            column = target - source + 1
            keep = (t - s == target - source) & (pattern[s, column] == 1) & (max(source, target) < counts[g])
            tile = s * 3 + column
            pair = target // 2
            row = source - pair
            lanes = slice(128 * (target % 2), 128 * (target % 2) + 128)
            for k, distance in enumerate(distances):
                z = my_z ^ distance
                for half in range(2):
                    quarter = ((my_xl ^ half) * 2 + z // 4) ^ my_q
                    for y in (0,) + PEERS:
                        if y == 0:
                            block = own[k][half, tile]
                        elif k <= len(NEAR):
                            block = first[PEERS.index(y)][g * pairs + n, k, half]
                        else:
                            block = second[PEERS.index(y)][g * pairs + n, k - 1 - len(NEAR), half]
                        weights[pair, row, quarter, z % 4, my_y ^ y, :, lanes] = jnp.where(keep, block, zero)

    total = jnp.zeros((CHUNK, 128), jnp.float32)
    left = [jnp.concatenate([q[0, l] for q in quarters], axis=1) for l in range(4)]
    for pair in range(2):
        acc = None
        for row in range(3):
            w = weights[pair, row].reshape(512, 256)
            part = jnp.dot(left[row + pair], w, preferred_element_type=jnp.float32)
            acc = part if acc is None else acc + part
        rounded = acc.astype(out.dtype)
        for m in range(2):
            mine = rounded[:, 128 * m : 128 * m + 128]
            out[0, 2 * pair + m] = mine
            wide = mine.astype(jnp.float32)
            total = total + wide * wide * occupation[pl.ds(slots[g, 2 * pair + m], 1), :]
    density[0] = lax.dot_general(
        jnp.ones((8, 128), jnp.float32), total, (((1,), (1,)), ((), ())),
        precision=lax.Precision.HIGHEST, preferred_element_type=jnp.float32,
    )[:1]


def rotate(meta, slot_ids, slot_count, pattern, own, first, second, occupation, quarters):
    blocks, slots_per, points, width = quarters[0].shape
    smem = pl.BlockSpec(memory_space=pltpu.SMEM)
    vmem = pl.BlockSpec(memory_space=pltpu.VMEM)
    tile = pl.BlockSpec((1, slots_per, CHUNK, width), lambda g, p: (g, 0, p, 0))
    return pl.pallas_call(
        rotate_kernel,
        grid=(blocks, points // CHUNK),
        out_shape=[
            jax.ShapeDtypeStruct(quarters[0].shape, quarters[0].dtype),
            jax.ShapeDtypeStruct((blocks, 1, points), jnp.float32),
        ],
        in_specs=[smem] * 4 + [vmem] * (len(own) + len(first) + len(second) + 1) + [tile] * 4,
        out_specs=[tile, pl.BlockSpec((1, 1, CHUNK), lambda g, p: (g, 0, p))],
        scratch_shapes=[pltpu.VMEM((2, 3, 4, 4, 4, 8, 256), jnp.bfloat16)],
        compiler_params=pltpu.CompilerParams(dimension_semantics=("arbitrary", "arbitrary")),
        cost_estimate=pl.CostEstimate(flops=3 * 10**9, bytes_accessed=14 * 10**6, transcendentals=0),
    )(meta, slot_ids, slot_count, pattern, *own, *first, *second, occupation, *quarters)


def body(orbitals, slot_ids, slot_count, band_tiles, pattern, occupation):
    rows = band_tiles.shape[2]
    meta = jnp.stack(
        [lax.axis_index("xl"), lax.axis_index("z"), lax.axis_index("y"), lax.axis_index("xh") * 2 + lax.axis_index("c")]
    ).astype(jnp.int32)
    tiles = band_tiles.reshape(-1, rows, band_tiles.shape[3])
    here = jnp.stack([tiles, swap(tiles, "xl")])
    far_half = swap(orbitals, "xh")
    near_half = swap(orbitals, "c")
    slots = [swap(slot_ids, "y", k) for k in PEERS]
    near = [here] + [swap(here, "z", k) for k in NEAR]
    far = [swap(here, "z", k) for k in FAR]
    packed = pack(slots, near)
    first = [swap(x, "y", k) for x, k in zip(packed, PEERS)]
    packed = pack(slots, far)
    second = [swap(x, "y", k) for x, k in zip(packed, PEERS)]
    quarters = [orbitals, near_half, far_half, swap(far_half, "c")]
    rotated, partial = rotate(meta, slot_ids, slot_count, pattern, near + far, first, second, occupation, quarters)
    partial = partial[:, 0]
    chip = partial + swap(partial, "c")
    return rotated, chip + swap(chip, "xh")


def solution(mesh):
    sizes = (2, 8, 4, 2, 2)
    torus = Mesh(mesh.devices.reshape(sizes), DOM + ORB)
    return jax.shard_map(
        body,
        mesh=torus,
        in_specs=(
            P(DOM, None, None, ORB),
            P(DOM, None),
            P(DOM),
            P(None, None, DOM, ORB),
            P(),
            P(None, ORB),
        ),
        out_specs=(P(DOM, None, None, ORB), P(DOM, None)),
        check_vma=False,
    )
```

time: 223 us -> 160 us (0.72)
  waiting for transfers between devices: 166 us -> 93.9 us
  starting transfers between devices: 3.61 us -> 40 us
  Pallas kernels: 0 us -> 17.5 us
  local copies, waits for them, and re-layouts: 18.7 us -> 4.36 us
  between operations: 13.8 us -> 0.73 us
  matrix products: 12.5 us -> 0 us
  blocking collectives: 6.49 us -> 0 us
    all_gather x3 -> x0, waiting for transfers between devices: 163 us -> none  [the longest x2 108 us: all_blocks(): tiles = lax.all_gather(tiles, axes[k])]
    ppermute x0 -> x22, waiting for transfers between devices: none -> 93.9 us  [swap(): return lax.ppermute(x, axis, [(i, i ^ distance) for i in range(size)])]
    ppermute x0 -> x22, starting transfers between devices: none -> 40 us  [swap(): return lax.ppermute(x, axis, [(i, i ^ distance) for i in range(size)])]
    pallas_call x0 -> x3, Pallas kernels: none -> 17.5 us  [the longest x1 12.8 us: rotate(): pl.pallas_call(rotate_kernel, grid=(blocks, points // CHUNK), out_shape=[...]
    dot_general x3 -> x0, matrix products: 12.5 us -> none  [the longest x1 9.84 us: rotate(): jnp.einsum('glpi,glmij->gmpj', values, tile_set, preferred_element_type=j...]
    gather x2 -> x0, local copies, waits for them, and re-layouts: 6.59 us -> none  [the longest x1 5.83 us: select_tiles(): picked = band_full[source, column]]
    all_gather x1 -> x0, blocking collectives: 6.49 us -> none  [all_blocks(): tiles = lax.all_gather(tiles, axes[k])]
    reshape x1 -> x0, local copies, waits for them, and re-layouts: 4.87 us -> none  [laid_out(): return jnp.moveaxis(tiles, 0, dim).reshape(shape)]
  transfers between devices with their start and end apart: 4 -> 22, of which waited for: 4 -> 13; matrix products, arithmetic and copies ran while one was open for 9% -> 2% of each run, Pallas kernels for 0% -> 3%
where the time goes in v1:
time: 160 us; the launch traced here: 159 us
  waiting for transfers between devices  93.9 us (59%)
  starting transfers between devices  40 us (25%)
  Pallas kernels  17.5 us (11%)
  local copies, waits for them, and re-layouts  4.36 us (3%)
  other arithmetic  2.87 us (2%)
    ppermute x22, waiting for transfers between devices, swap(): return lax.ppermute(x, axis, [(i, i ^ distance) for i in range(size)])  93.9 us
    ppermute x22, starting transfers between devices, swap(): return lax.ppermute(x, axis, [(i, i ^ distance) for i in range(size)])  40 us
    pallas_call x1, Pallas kernels, rotate(): pl.pallas_call(rotate_kernel, grid=(blocks, points // CHUNK), out_shape=[...  12.8 us
    pallas_call x2, Pallas kernels, pack(): pl.pallas_call(pack_kernel, out_shape=[shape] * len(slots), in_specs=[sme...  4.71 us
    unnamed x34, local copies, waits for them, and re-layouts  4.36 us
  transfers between devices with their start and end apart: 22, of which 13 were waited for; matrix products, arithmetic and copies ran while one was open for 2% of the time, Pallas kernels for 3%

profile of v1, /device:TPU:1, one launch (start us, length us, event | category | flops | bytes accessed | tf_op | source)
XLA Modules:
  0.0 159.4 jit_solution(5389924908337860036)
XLA Ops:
  0.6 3.6 %collective-permute-start.18 = (bf16[2,4,1024,128]{3,2,1,0:T(8,128)(2,1)}, bf16[2,4,1024,128]{3,2,1,0:T(8,128)(2,1)S(1)}, u32[]{:S(2)}, u32[]{:S(2)}) collective-permute-start(bf16[2,4,1024,128]{3,2,1,0:T(8,128)(2,1)} %refs_15_.1), channel_id=1, source_target_pairs={{0,2},{2,0},{1,3},{3,1},{4,6},{6,4},{5,7},{7,5},{8,10},{10,8},{9,1... | collective-permute-start | bytes 6291464 | tf_op jit(solution)/shard_map/ppermute | solution.py:22
  4.3 1.0 collective-permute-start.17
  5.2 43.7 %collective-permute-done.18.refs_17_ = bf16[2,4,1024,128]{3,2,1,0:T(8,128)(2,1)S(1)} collective-permute-done((bf16[2,4,1024,128]{3,2,1,0:T(8,128)(2,1)}, bf16[2,4,1024,128]{3,2,1,0:T(8,128)(2,1)S(1)}, u32[]{:S(2)}, u32[]{:S(2)}) %collective-permute-start.18) | collective-permute-done | bytes 2097184 | tf_op jit(solution)/shard_map/ppermute | solution.py:22
  48.9 2.2 %collective-permute-start.19 = (bf16[2,4,1024,128]{3,2,1,0:T(8,128)(2,1)S(1)}, bf16[2,4,1024,128]{3,2,1,0:T(8,128)(2,1)}, u32[]{:S(2)}, u32[]{:S(2)}) collective-permute-start(bf16[2,4,1024,128]{3,2,1,0:T(8,128)(2,1)S(1)} %collective-permute-done.18.refs_17_), channel_id=1, source_target_pairs={{0,1},{1,0},{2,3},{3,2},{4,5},{5,4},{6,7},{7,6},{8,9},{9,8},{10,11... | collective-permute-start | bytes 6291464 | tf_op jit(solution)/shard_map/ppermute | solution.py:22
  51.1 1.4 collective-permute-start
  52.5 3.1 %collective-permute-done = bf16[48,8,128]{2,1,0:T(8,128)(2,1)S(1)} collective-permute-done((bf16[48,8,128]{2,1,0:T(8,128)(2,1)}, bf16[48,8,128]{2,1,0:T(8,128)(2,1)S(1)}, u32[]{:S(2)}, u32[]{:S(2)}) %collective-permute-start) | collective-permute-done | bytes 98336 | tf_op jit(solution)/shard_map/ppermute | solution.py:22
  55.6 0.9 pad_maximum_fusion.refs_3_.refs_0_
  56.6 0.0 copy-start.1
  56.6 7.2 %collective-permute-start.7 = (bf16[2,48,8,128]{3,2,1,0:T(8,128)(2,1)S(1)}, bf16[2,48,8,128]{3,2,1,0:T(8,128)(2,1)S(1)}, u32[]{:S(2)}, u32[]{:S(2)}) collective-permute-start(bf16[2,48,8,128]{3,2,1,0:T(8,128)(2,1)S(1)} %pad_maximum_fusion.refs_3_.refs_0_), channel_id=1, source_target_pairs={{0,64},{16,80},{32,96},{48,112},{64,0},{80,16},{96,32},{112,48},{1... | collective-permute-start | bytes 589832 | tf_op jit(solution)/shard_map/ppermute | solution.py:22
  63.8 2.7 %collective-permute-start.9 = (s32[2,4]{1,0:T(2,128)}, s32[2,4]{1,0:T(2,128)S(1)}, u32[]{:S(2)}, u32[]{:S(2)}) collective-permute-start(s32[2,4]{1,0:T(2,128)} %slots.1), channel_id=1, source_target_pairs={{0,12},{4,8},{8,4},{12,0},{1,13},{5,9},{9,5},{13,1},{2,14},{6,10},... | collective-permute-start | bytes 104 | tf_op jit(solution)/shard_map/ppermute | solution.py:22
  66.5 0.0 collective-permute-start.8
  66.5 1.5 collective-permute-done.9.refs_1_
  68.0 0.0 collective-permute-start.6
  68.0 1.5 collective-permute-done.8.refs_0_
  69.4 0.3 collective-permute-start.10
  69.8 3.8 %collective-permute-done.10.refs_2_ = s32[2,4]{1,0:T(2,128)S(1)} collective-permute-done((s32[2,4]{1,0:T(2,128)}, s32[2,4]{1,0:T(2,128)S(1)}, u32[]{:S(2)}, u32[]{:S(2)}) %collective-permute-start.10) | collective-permute-done | bytes 64 | tf_op jit(solution)/shard_map/ppermute | solution.py:22
  73.6 2.9 %collective-permute-start.5 = (bf16[2,48,8,128]{3,2,1,0:T(8,128)(2,1)S(1)}, bf16[2,48,8,128]{3,2,1,0:T(8,128)(2,1)S(1)}, u32[]{:S(2)}, u32[]{:S(2)}) collective-permute-start(bf16[2,48,8,128]{3,2,1,0:T(8,128)(2,1)S(1)} %pad_maximum_fusion.refs_3_.refs_0_), channel_id=1, source_target_pairs={{0,96},{16,112},{32,64},{48,80},{64,32},{80,48},{96,0},{112,16},{1... | collective-permute-start | bytes 589832 | tf_op jit(solution)/shard_map/ppermute | solution.py:22
  76.5 0.0 collective-permute-done.7.refs_5_.refs_7_
  76.5 1.2 collective-permute-start.4
  77.6 10.5 %collective-permute-done.6.refs_4_.refs_6_ = bf16[2,48,8,128]{3,2,1,0:T(8,128)(2,1)S(1)} collective-permute-done((bf16[2,48,8,128]{3,2,1,0:T(8,128)(2,1)S(1)}, bf16[2,48,8,128]{3,2,1,0:T(8,128)(2,1)S(1)}, u32[]{:S(2)}, u32[]{:S(2)}) %collective-permute-start.6) | collective-permute-done | bytes 196640 | tf_op jit(solution)/shard_map/ppermute | solution.py:22
  88.1 0.0 collective-permute-start.3
  88.1 1.8 %collective-permute-done.5.refs_3_.refs_5_ = bf16[2,48,8,128]{3,2,1,0:T(8,128)(2,1)S(1)} collective-permute-done((bf16[2,48,8,128]{3,2,1,0:T(8,128)(2,1)S(1)}, bf16[2,48,8,128]{3,2,1,0:T(8,128)(2,1)S(1)}, u32[]{:S(2)}, u32[]{:S(2)}) %collective-permute-start.5) | collective-permute-done | bytes 196640 | tf_op jit(solution)/shard_map/ppermute | solution.py:22
  89.9 1.6 %collective-permute-start.2 = (bf16[2,48,8,128]{3,2,1,0:T(8,128)(2,1)S(1)}, bf16[2,48,8,128]{3,2,1,0:T(8,128)(2,1)S(1)}, u32[]{:S(2)}, u32[]{:S(2)}) collective-permute-start(bf16[2,48,8,128]{3,2,1,0:T(8,128)(2,1)S(1)} %pad_maximum_fusion.refs_3_.refs_0_), channel_id=1, source_target_pairs={{0,48},{16,32},{32,16},{48,0},{64,112},{80,96},{96,80},{112,64},{1... | collective-permute-start | bytes 589832 | tf_op jit(solution)/shard_map/ppermute | solution.py:22
  91.6 0.0 collective-permute-done.4.refs_7_.refs_4_
  91.6 0.8 collective-permute-start.1
  92.4 0.0 copy-done.13
  92.4 0.0 copy-done.3
  92.4 0.0 copy-done.4
  92.4 2.2 %shard_map.78 = (bf16[20,3,2,8,128]{4,3,2,1,0:T(8,128)(2,1)}, bf16[20,3,2,8,128]{4,3,2,1,0:T(8,128)(2,1)}, bf16[20,3,2,8,128]{4,3,2,1,0:T(8,128)(2,1)}) custom-call(s32[2,4]{1,0:T(2,128)} %copy-done.14, s32[2,4]{1,0:T(2,128)} %copy-done.13, s32[2,4]{1,0:T(2,128)} %copy-done.15, bf16[2,48,8,128]{3,2,1,0:T(8,128)(2,1)} %copy-done.4, ...), custom_call_target="tpu_custom_call" | custom-call | flops 1000000 | bytes 2000000 | tf_op jit(solution)/shard_map/pallas_call | solution.py:41
  94.6 1.6 %collective-permute-done.3.refs_6_.refs_3_ = bf16[2,48,8,128]{3,2,1,0:T(8,128)(2,1)S(1)} collective-permute-done((bf16[2,48,8,128]{3,2,1,0:T(8,128)(2,1)S(1)}, bf16[2,48,8,128]{3,2,1,0:T(8,128)(2,1)S(1)}, u32[]{:S(2)}, u32[]{:S(2)}) %collective-permute-start.3) | collective-permute-done | bytes 196640 | tf_op jit(solution)/shard_map/ppermute | solution.py:22
  96.2 2.4 %collective-permute-start.14 = (bf16[20,3,2,8,128]{4,3,2,1,0:T(8,128)(2,1)}, bf16[20,3,2,8,128]{4,3,2,1,0:T(8,128)(2,1)S(1)}, u32[]{:S(2)}, u32[]{:S(2)}) collective-permute-start(bf16[20,3,2,8,128]{4,3,2,1,0:T(8,128)(2,1)} %get-tuple-element.13), channel_id=1, source_target_pairs={{0,4},{4,0},{8,12},{12,8},{1,5},{5,1},{9,13},{13,9},{2,6},{6,2},{1... | collective-permute-start | bytes 737288 | tf_op jit(solution)/shard_map/ppermute | solution.py:22
  98.6 3.9 %collective-permute-done.2.refs_5_.refs_2_ = bf16[2,48,8,128]{3,2,1,0:T(8,128)(2,1)S(1)} collective-permute-done((bf16[2,48,8,128]{3,2,1,0:T(8,128)(2,1)S(1)}, bf16[2,48,8,128]{3,2,1,0:T(8,128)(2,1)S(1)}, u32[]{:S(2)}, u32[]{:S(2)}) %collective-permute-start.2) | collective-permute-done | bytes 196640 | tf_op jit(solution)/shard_map/ppermute | solution.py:22
  102.5 2.7 %collective-permute-start.15 = (bf16[20,3,2,8,128]{4,3,2,1,0:T(8,128)(2,1)}, bf16[20,3,2,8,128]{4,3,2,1,0:T(8,128)(2,1)S(1)}, u32[]{:S(2)}, u32[]{:S(2)}) collective-permute-start(bf16[20,3,2,8,128]{4,3,2,1,0:T(8,128)(2,1)} %get-tuple-element.14), channel_id=1, source_target_pairs={{0,12},{4,8},{8,4},{12,0},{1,13},{5,9},{9,5},{13,1},{2,14},{6,10},... | collective-permute-start | bytes 737288 | tf_op jit(solution)/shard_map/ppermute | solution.py:22
  105.2 0.0 collective-permute-done.1.refs_4_.refs_1_
  105.2 2.4 %collective-permute-start.16 = (bf16[20,3,2,8,128]{4,3,2,1,0:T(8,128)(2,1)}, bf16[20,3,2,8,128]{4,3,2,1,0:T(8,128)(2,1)}, u32[]{:S(2)}, u32[]{:S(2)}) collective-permute-start(bf16[20,3,2,8,128]{4,3,2,1,0:T(8,128)(2,1)} %get-tuple-element.15), channel_id=1, source_target_pairs={{0,8},{4,12},{8,0},{12,4},{1,9},{5,13},{9,1},{13,5},{2,10},{6,14},... | collective-permute-start | bytes 737288 | tf_op jit(solution)/shard_map/ppermute | solution.py:22
  107.6 0.0 copy-done.6
  107.6 2.6 %shard_map.77 = (bf16[20,5,2,8,128]{4,3,2,1,0:T(8,128)(2,1)}, bf16[20,5,2,8,128]{4,3,2,1,0:T(8,128)(2,1)}, bf16[20,5,2,8,128]{4,3,2,1,0:T(8,128)(2,1)}) custom-call(s32[2,4]{1,0:T(2,128)} %copy-done.14, s32[2,4]{1,0:T(2,128)} %copy-done.13, s32[2,4]{1,0:T(2,128)} %copy-done.15, bf16[2,48,8,128]{3,2,1,0:T(8,128)(2,1)} %copy-done.1, ...), custom_call_target="tpu_custom_call" | custom-call | flops 1000000 | bytes 2000000 | tf_op jit(solution)/shard_map/pallas_call | solution.py:41
  110.1 0.0 collective-permute-done.14.refs_11_
  110.1 0.7 copy-done.11
  110.8 0.0 collective-permute-start.11
  110.8 5.2 %collective-permute-done.15.refs_12_ = bf16[20,3,2,8,128]{4,3,2,1,0:T(8,128)(2,1)S(1)} collective-permute-done((bf16[20,3,2,8,128]{4,3,2,1,0:T(8,128)(2,1)}, bf16[20,3,2,8,128]{4,3,2,1,0:T(8,128)(2,1)S(1)}, u32[]{:S(2)}, u32[]{:S(2)}) %collective-permute-start.15) | collective-permute-done | bytes 245792 | tf_op jit(solution)/shard_map/ppermute | solution.py:22
  116.1 0.7 copy-done.12
  116.8 2.7 %collective-permute-start.12 = (bf16[20,5,2,8,128]{4,3,2,1,0:T(8,128)(2,1)}, bf16[20,5,2,8,128]{4,3,2,1,0:T(8,128)(2,1)S(1)}, u32[]{:S(2)}, u32[]{:S(2)}) collective-permute-start(bf16[20,5,2,8,128]{4,3,2,1,0:T(8,128)(2,1)} %get-tuple-element.11), channel_id=1, source_target_pairs={{0,12},{4,8},{8,4},{12,0},{1,13},{5,9},{9,5},{13,1},{2,14},{6,10},... | collective-permute-start | bytes 1228808 | tf_op jit(solution)/shard_map/ppermute | solution.py:22
  119.5 0.0 collective-permute-done.16.refs_13_
  119.5 0.0 collective-permute-start.13
  119.5 1.4 copy.8.pattern
  120.8 0.6 pad_add_fusion.meta
  121.5 0.0 collective-permute-done.11.refs_8_
  121.5 15.2 %collective-permute-done.12.refs_9_ = bf16[20,5,2,8,128]{4,3,2,1,0:T(8,128)(2,1)S(1)} collective-permute-done((bf16[20,5,2,8,128]{4,3,2,1,0:T(8,128)(2,1)}, bf16[20,5,2,8,128]{4,3,2,1,0:T(8,128)(2,1)S(1)}, u32[]{:S(2)}, u32[]{:S(2)}) %collective-permute-start.12) | collective-permute-done | bytes 409632 | tf_op jit(solution)/shard_map/ppermute | solution.py:22
  136.7 0.0 collective-permute-done.13.refs_10_
  136.7 0.0 collective-permute-done.17.refs_16_
  136.7 0.0 collective-permute-done.19.refs_18_
  136.7 0.0 copy-done
  136.7 0.0 copy-done.8
  136.8 0.7 copy-done.9
  137.5 0.1 copy-done.10
  137.6 12.8 %shard_map.79 = (bf16[2,4,1024,128]{3,2,1,0:T(8,128)(2,1)}, f32[2,1,1024]{2,1,0:T(1,128)}) custom-call(s32[4]{0:T(128)} %pad_add_fusion.meta, s32[2,4]{1,0:T(2,128)} %slots.1, s32[2]{0:T(128)} %counts.1, s32[16,3]{1,0:T(8,128)} %copy.8.pattern, bf16[2,48,8,128]{3,2,1,0:T(8,128)(2,1)} %copy-done.1, ...), custom_call_target="tpu_custom_call" | custom-call | flops 3000000000 | bytes 14000000 | tf_op jit(solution)/shard_map/pallas_call | solution.py:112
  150.4 0.7 copy.13
  151.1 2.2 %collective-permute-start.20 = (f32[2,1024]{1,0:T(2,128)S(1)}, f32[2,1024]{1,0:T(2,128)S(1)}, u32[]{:S(2)}, u32[]{:S(2)}) collective-permute-start(f32[2,1024]{1,0:T(2,128)S(1)} %bitcast.15), channel_id=1, source_target_pairs={{0,1},{1,0},{2,3},{3,2},{4,5},{5,4},{6,7},{7,6},{8,9},{9,8},{10,11... | collective-permute-start | bytes 24584 | tf_op jit(solution)/shard_map/ppermute | solution.py:22
  153.2 0.8 collective-permute-done.20
  154.1 0.7 fusion
  154.8 2.7 %collective-permute-start.21 = (f32[2,1024]{1,0:T(2,128)S(1)}, f32[2,1024]{1,0:T(2,128)S(1)}, u32[]{:S(2)}, u32[]{:S(2)}) collective-permute-start(f32[2,1024]{1,0:T(2,128)S(1)} %fusion), channel_id=1, source_target_pairs={{0,2},{2,0},{1,3},{3,1},{4,6},{6,4},{5,7},{7,5},{8,10},{10,8},{9,1... | collective-permute-start | bytes 24584 | tf_op jit(solution)/shard_map/ppermute | solution.py:22
  157.5 1.3 collective-permute-done.21
  158.8 0.6 add.11
  (21 shorter events, 0.0 us)
Async XLA Ops:
  0.6 48.3 %collective-permute-start.18 = (bf16[2,4,1024,128]{3,2,1,0:T(8,128)(2,1)}, bf16[2,4,1024,128]{3,2,1,0:T(8,128)(2,1)S(1)}, u32[]{:S(2)}, u32[]{:S(2)}) collective-permute-start(bf16[2,4,1024,128]{3,2,1,0:T(8,128)(2,1)} %refs_15_.1), channel_id=1, source_target_pairs={{0,2},{2,0},{1,3},{3,1},{4,6},{6,4},{5,7},{7,5},{8,10},{10,8},{9,1... | collective-permute-start | bytes 6291464 | tf_op jit(solution)/shard_map/ppermute | solution.py:22
  4.3 132.4 %collective-permute-start.17 = (bf16[2,4,1024,128]{3,2,1,0:T(8,128)(2,1)}, bf16[2,4,1024,128]{3,2,1,0:T(8,128)(2,1)}, u32[]{:S(2)}, u32[]{:S(2)}) collective-permute-start(bf16[2,4,1024,128]{3,2,1,0:T(8,128)(2,1)} %refs_15_.1), channel_id=1, source_target_pairs={{0,1},{1,0},{2,3},{3,2},{4,5},{5,4},{6,7},{7,6},{8,9},{9,8},{10,11... | collective-permute-start | bytes 6291464 | tf_op jit(solution)/shard_map/ppermute | solution.py:22
  48.9 87.8 %copy-start = (bf16[2,4,1024,128]{3,2,1,0:T(8,128)(2,1)}, bf16[2,4,1024,128]{3,2,1,0:T(8,128)(2,1)S(1)}, u32[]{:S(2)}) copy-start(bf16[2,4,1024,128]{3,2,1,0:T(8,128)(2,1)S(1)} %collective-permute-done.18.refs_17_) | copy-start | bytes 6291460
  48.9 87.8 %collective-permute-start.19 = (bf16[2,4,1024,128]{3,2,1,0:T(8,128)(2,1)S(1)}, bf16[2,4,1024,128]{3,2,1,0:T(8,128)(2,1)}, u32[]{:S(2)}, u32[]{:S(2)}) collective-permute-start(bf16[2,4,1024,128]{3,2,1,0:T(8,128)(2,1)S(1)} %collective-permute-done.18.refs_17_), channel_id=1, source_target_pairs={{0,1},{1,0},{2,3},{3,2},{4,5},{5,4},{6,7},{7,6},{8,9},{9,8},{10,11... | collective-permute-start | bytes 6291464 | tf_op jit(solution)/shard_map/ppermute | solution.py:22
  51.1 4.6 %collective-permute-start = (bf16[48,8,128]{2,1,0:T(8,128)(2,1)}, bf16[48,8,128]{2,1,0:T(8,128)(2,1)S(1)}, u32[]{:S(2)}, u32[]{:S(2)}) collective-permute-start(bf16[48,8,128]{2,1,0:T(8,128)(2,1)} %bitcast.12), channel_id=1, source_target_pairs={{0,128},{128,0},{1,129},{129,1},{2,130},{130,2},{3,131},{131,3},{4... | collective-permute-start | bytes 294920 | tf_op jit(solution)/shard_map/ppermute | solution.py:22
  56.6 51.0 %copy-start.1 = (bf16[2,48,8,128]{3,2,1,0:T(8,128)(2,1)}, bf16[2,48,8,128]{3,2,1,0:T(8,128)(2,1)S(1)}, u32[]{:S(2)}) copy-start(bf16[2,48,8,128]{3,2,1,0:T(8,128)(2,1)S(1)} %pad_maximum_fusion.refs_3_.refs_0_) | copy-start | bytes 589828
  56.6 19.9 %collective-permute-start.7 = (bf16[2,48,8,128]{3,2,1,0:T(8,128)(2,1)S(1)}, bf16[2,48,8,128]{3,2,1,0:T(8,128)(2,1)S(1)}, u32[]{:S(2)}, u32[]{:S(2)}) collective-permute-start(bf16[2,48,8,128]{3,2,1,0:T(8,128)(2,1)S(1)} %pad_maximum_fusion.refs_3_.refs_0_), channel_id=1, source_target_pairs={{0,64},{16,80},{32,96},{48,112},{64,0},{80,16},{96,32},{112,48},{1... | collective-permute-start | bytes 589832 | tf_op jit(solution)/shard_map/ppermute | solution.py:22
  63.8 4.2 %collective-permute-start.9 = (s32[2,4]{1,0:T(2,128)}, s32[2,4]{1,0:T(2,128)S(1)}, u32[]{:S(2)}, u32[]{:S(2)}) collective-permute-start(s32[2,4]{1,0:T(2,128)} %slots.1), channel_id=1, source_target_pairs={{0,12},{4,8},{8,4},{12,0},{1,13},{5,9},{9,5},{13,1},{2,14},{6,10},... | collective-permute-start | bytes 104 | tf_op jit(solution)/shard_map/ppermute | solution.py:22
  66.5 2.9 %collective-permute-start.8 = (s32[2,4]{1,0:T(2,128)}, s32[2,4]{1,0:T(2,128)S(1)}, u32[]{:S(2)}, u32[]{:S(2)}) collective-permute-start(s32[2,4]{1,0:T(2,128)} %slots.1), channel_id=1, source_target_pairs={{0,4},{4,0},{8,12},{12,8},{1,5},{5,1},{9,13},{13,9},{2,6},{6,2},{1... | collective-permute-start | bytes 104 | tf_op jit(solution)/shard_map/ppermute | solution.py:22
  68.0 24.4 %copy-start.13 = (s32[2,4]{1,0:T(2,128)}, s32[2,4]{1,0:T(2,128)S(1)}, u32[]{:S(2)}) copy-start(s32[2,4]{1,0:T(2,128)S(1)} %collective-permute-done.9.refs_1_) | copy-start | bytes 100
  68.0 20.1 %collective-permute-start.6 = (bf16[2,48,8,128]{3,2,1,0:T(8,128)(2,1)S(1)}, bf16[2,48,8,128]{3,2,1,0:T(8,128)(2,1)S(1)}, u32[]{:S(2)}, u32[]{:S(2)}) collective-permute-start(bf16[2,48,8,128]{3,2,1,0:T(8,128)(2,1)S(1)} %pad_maximum_fusion.refs_3_.refs_0_), channel_id=1, source_target_pairs={{0,80},{16,64},{32,112},{48,96},{64,16},{80,0},{96,48},{112,32},{1... | collective-permute-start | bytes 589832 | tf_op jit(solution)/shard_map/ppermute | solution.py:22
  69.4 23.0 %copy-start.14 = (s32[2,4]{1,0:T(2,128)}, s32[2,4]{1,0:T(2,128)S(1)}, u32[]{:S(2)}) copy-start(s32[2,4]{1,0:T(2,128)S(1)} %collective-permute-done.8.refs_0_) | copy-start | bytes 100
  69.4 4.1 %collective-permute-start.10 = (s32[2,4]{1,0:T(2,128)}, s32[2,4]{1,0:T(2,128)S(1)}, u32[]{:S(2)}, u32[]{:S(2)}) collective-permute-start(s32[2,4]{1,0:T(2,128)} %slots.1), channel_id=1, source_target_pairs={{0,8},{4,12},{8,0},{12,4},{1,9},{5,13},{9,1},{13,5},{2,10},{6,14},... | collective-permute-start | bytes 104 | tf_op jit(solution)/shard_map/ppermute | solution.py:22
  73.6 18.8 %copy-start.15 = (s32[2,4]{1,0:T(2,128)}, s32[2,4]{1,0:T(2,128)S(1)}, u32[]{:S(2)}) copy-start(s32[2,4]{1,0:T(2,128)S(1)} %collective-permute-done.10.refs_2_) | copy-start | bytes 100
  73.6 16.3 %collective-permute-start.5 = (bf16[2,48,8,128]{3,2,1,0:T(8,128)(2,1)S(1)}, bf16[2,48,8,128]{3,2,1,0:T(8,128)(2,1)S(1)}, u32[]{:S(2)}, u32[]{:S(2)}) collective-permute-start(bf16[2,48,8,128]{3,2,1,0:T(8,128)(2,1)S(1)} %pad_maximum_fusion.refs_3_.refs_0_), channel_id=1, source_target_pairs={{0,96},{16,112},{32,64},{48,80},{64,32},{80,48},{96,0},{112,16},{1... | collective-permute-start | bytes 589832 | tf_op jit(solution)/shard_map/ppermute | solution.py:22
  76.5 15.9 %copy-start.2 = (bf16[2,48,8,128]{3,2,1,0:T(8,128)(2,1)}, bf16[2,48,8,128]{3,2,1,0:T(8,128)(2,1)S(1)}, u32[]{:S(2)}) copy-start(bf16[2,48,8,128]{3,2,1,0:T(8,128)(2,1)S(1)} %collective-permute-done.7.refs_5_.refs_7_) | copy-start | bytes 589828
  76.5 15.1 %collective-permute-start.4 = (bf16[2,48,8,128]{3,2,1,0:T(8,128)(2,1)S(1)}, bf16[2,48,8,128]{3,2,1,0:T(8,128)(2,1)S(1)}, u32[]{:S(2)}, u32[]{:S(2)}) collective-permute-start(bf16[2,48,8,128]{3,2,1,0:T(8,128)(2,1)S(1)} %pad_maximum_fusion.refs_3_.refs_0_), channel_id=1, source_target_pairs={{0,32},{16,48},{32,0},{48,16},{64,96},{80,112},{96,64},{112,80},{1... | collective-permute-start | bytes 589832 | tf_op jit(solution)/shard_map/ppermute | solution.py:22
  88.1 4.3 %copy-start.3 = (bf16[2,48,8,128]{3,2,1,0:T(8,128)(2,1)}, bf16[2,48,8,128]{3,2,1,0:T(8,128)(2,1)S(1)}, u32[]{:S(2)}) copy-start(bf16[2,48,8,128]{3,2,1,0:T(8,128)(2,1)S(1)} %collective-permute-done.6.refs_4_.refs_6_) | copy-start | bytes 589828
  88.1 8.1 %collective-permute-start.3 = (bf16[2,48,8,128]{3,2,1,0:T(8,128)(2,1)S(1)}, bf16[2,48,8,128]{3,2,1,0:T(8,128)(2,1)S(1)}, u32[]{:S(2)}, u32[]{:S(2)}) collective-permute-start(bf16[2,48,8,128]{3,2,1,0:T(8,128)(2,1)S(1)} %pad_maximum_fusion.refs_3_.refs_0_), channel_id=1, source_target_pairs={{0,112},{16,96},{32,80},{48,64},{64,48},{80,32},{96,16},{112,0},{1... | collective-permute-start | bytes 589832 | tf_op jit(solution)/shard_map/ppermute | solution.py:22
  89.9 2.5 %copy-start.4 = (bf16[2,48,8,128]{3,2,1,0:T(8,128)(2,1)}, bf16[2,48,8,128]{3,2,1,0:T(8,128)(2,1)S(1)}, u32[]{:S(2)}) copy-start(bf16[2,48,8,128]{3,2,1,0:T(8,128)(2,1)S(1)} %collective-permute-done.5.refs_3_.refs_5_) | copy-start | bytes 589828
  89.9 12.6 %collective-permute-start.2 = (bf16[2,48,8,128]{3,2,1,0:T(8,128)(2,1)S(1)}, bf16[2,48,8,128]{3,2,1,0:T(8,128)(2,1)S(1)}, u32[]{:S(2)}, u32[]{:S(2)}) collective-permute-start(bf16[2,48,8,128]{3,2,1,0:T(8,128)(2,1)S(1)} %pad_maximum_fusion.refs_3_.refs_0_), channel_id=1, source_target_pairs={{0,48},{16,32},{32,16},{48,0},{64,112},{80,96},{96,80},{112,64},{1... | collective-permute-start | bytes 589832 | tf_op jit(solution)/shard_map/ppermute | solution.py:22
  91.6 16.0 %copy-start.5 = (bf16[2,48,8,128]{3,2,1,0:T(8,128)(2,1)}, bf16[2,48,8,128]{3,2,1,0:T(8,128)(2,1)S(1)}, u32[]{:S(2)}) copy-start(bf16[2,48,8,128]{3,2,1,0:T(8,128)(2,1)S(1)} %collective-permute-done.4.refs_7_.refs_4_) | copy-start | bytes 589828
  91.6 13.6 %collective-permute-start.1 = (bf16[2,48,8,128]{3,2,1,0:T(8,128)(2,1)S(1)}, bf16[2,48,8,128]{3,2,1,0:T(8,128)(2,1)}, u32[]{:S(2)}, u32[]{:S(2)}) collective-permute-start(bf16[2,48,8,128]{3,2,1,0:T(8,128)(2,1)S(1)} %pad_maximum_fusion.refs_3_.refs_0_), channel_id=1, source_target_pairs={{0,16},{16,0},{32,48},{48,32},{64,80},{80,64},{96,112},{112,96},{1... | collective-permute-start | bytes 589832 | tf_op jit(solution)/shard_map/ppermute | solution.py:22
  96.2 11.4 %copy-start.6 = (bf16[2,48,8,128]{3,2,1,0:T(8,128)(2,1)}, bf16[2,48,8,128]{3,2,1,0:T(8,128)(2,1)S(1)}, u32[]{:S(2)}) copy-start(bf16[2,48,8,128]{3,2,1,0:T(8,128)(2,1)S(1)} %collective-permute-done.3.refs_6_.refs_3_) | copy-start | bytes 589828
  96.2 13.9 %collective-permute-start.14 = (bf16[20,3,2,8,128]{4,3,2,1,0:T(8,128)(2,1)}, bf16[20,3,2,8,128]{4,3,2,1,0:T(8,128)(2,1)S(1)}, u32[]{:S(2)}, u32[]{:S(2)}) collective-permute-start(bf16[20,3,2,8,128]{4,3,2,1,0:T(8,128)(2,1)} %get-tuple-element.13), channel_id=1, source_target_pairs={{0,4},{4,0},{8,12},{12,8},{1,5},{5,1},{9,13},{13,9},{2,6},{6,2},{1... | collective-permute-start | bytes 737288 | tf_op jit(solution)/shard_map/ppermute | solution.py:22
  102.5 5.1 %copy-start.7 = (bf16[2,48,8,128]{3,2,1,0:T(8,128)(2,1)}, bf16[2,48,8,128]{3,2,1,0:T(8,128)(2,1)S(1)}, u32[]{:S(2)}) copy-start(bf16[2,48,8,128]{3,2,1,0:T(8,128)(2,1)S(1)} %collective-permute-done.2.refs_5_.refs_2_) | copy-start | bytes 589828
  102.5 13.6 %collective-permute-start.15 = (bf16[20,3,2,8,128]{4,3,2,1,0:T(8,128)(2,1)}, bf16[20,3,2,8,128]{4,3,2,1,0:T(8,128)(2,1)S(1)}, u32[]{:S(2)}, u32[]{:S(2)}) collective-permute-start(bf16[20,3,2,8,128]{4,3,2,1,0:T(8,128)(2,1)} %get-tuple-element.14), channel_id=1, source_target_pairs={{0,12},{4,8},{8,4},{12,0},{1,13},{5,9},{9,5},{13,1},{2,14},{6,10},... | collective-permute-start | bytes 737288 | tf_op jit(solution)/shard_map/ppermute | solution.py:22
  105.2 14.3 %collective-permute-start.16 = (bf16[20,3,2,8,128]{4,3,2,1,0:T(8,128)(2,1)}, bf16[20,3,2,8,128]{4,3,2,1,0:T(8,128)(2,1)}, u32[]{:S(2)}, u32[]{:S(2)}) collective-permute-start(bf16[20,3,2,8,128]{4,3,2,1,0:T(8,128)(2,1)} %get-tuple-element.15), channel_id=1, source_target_pairs={{0,8},{4,12},{8,0},{12,4},{1,9},{5,13},{9,1},{13,5},{2,10},{6,14},... | collective-permute-start | bytes 737288 | tf_op jit(solution)/shard_map/ppermute | solution.py:22
  110.1 0.7 copy-start.11
  110.8 10.6 %collective-permute-start.11 = (bf16[20,5,2,8,128]{4,3,2,1,0:T(8,128)(2,1)}, bf16[20,5,2,8,128]{4,3,2,1,0:T(8,128)(2,1)S(1)}, u32[]{:S(2)}, u32[]{:S(2)}) collective-permute-start(bf16[20,5,2,8,128]{4,3,2,1,0:T(8,128)(2,1)} %get-tuple-element.10), channel_id=1, source_target_pairs={{0,4},{4,0},{8,12},{12,8},{1,5},{5,1},{9,13},{13,9},{2,6},{6,2},{1... | collective-permute-start | bytes 1228808 | tf_op jit(solution)/shard_map/ppermute | solution.py:22
  116.1 0.7 copy-start.12
  116.8 19.9 %collective-permute-start.12 = (bf16[20,5,2,8,128]{4,3,2,1,0:T(8,128)(2,1)}, bf16[20,5,2,8,128]{4,3,2,1,0:T(8,128)(2,1)S(1)}, u32[]{:S(2)}, u32[]{:S(2)}) collective-permute-start(bf16[20,5,2,8,128]{4,3,2,1,0:T(8,128)(2,1)} %get-tuple-element.11), channel_id=1, source_target_pairs={{0,12},{4,8},{8,4},{12,0},{1,13},{5,9},{9,5},{13,1},{2,14},{6,10},... | collective-permute-start | bytes 1228808 | tf_op jit(solution)/shard_map/ppermute | solution.py:22
  119.5 17.3 %collective-permute-start.13 = (bf16[20,5,2,8,128]{4,3,2,1,0:T(8,128)(2,1)}, bf16[20,5,2,8,128]{4,3,2,1,0:T(8,128)(2,1)S(1)}, u32[]{:S(2)}, u32[]{:S(2)}) collective-permute-start(bf16[20,5,2,8,128]{4,3,2,1,0:T(8,128)(2,1)} %get-tuple-element.12), channel_id=1, source_target_pairs={{0,8},{4,12},{8,0},{12,4},{1,9},{5,13},{9,1},{13,5},{2,10},{6,14},... | collective-permute-start | bytes 1228808 | tf_op jit(solution)/shard_map/ppermute | solution.py:22
  121.5 15.3 %copy-start.8 = (bf16[20,5,2,8,128]{4,3,2,1,0:T(8,128)(2,1)}, bf16[20,5,2,8,128]{4,3,2,1,0:T(8,128)(2,1)S(1)}, u32[]{:S(2)}) copy-start(bf16[20,5,2,8,128]{4,3,2,1,0:T(8,128)(2,1)S(1)} %collective-permute-done.11.refs_8_) | copy-start | bytes 1228804
  136.7 0.8 copy-start.9
  136.7 0.9 copy-start.10
  151.1 3.0 %collective-permute-start.20 = (f32[2,1024]{1,0:T(2,128)S(1)}, f32[2,1024]{1,0:T(2,128)S(1)}, u32[]{:S(2)}, u32[]{:S(2)}) collective-permute-start(f32[2,1024]{1,0:T(2,128)S(1)} %bitcast.15), channel_id=1, source_target_pairs={{0,1},{1,0},{2,3},{3,2},{4,5},{5,4},{6,7},{7,6},{8,9},{9,8},{10,11... | collective-permute-start | bytes 24584 | tf_op jit(solution)/shard_map/ppermute | solution.py:22
  154.8 4.0 %collective-permute-start.21 = (f32[2,1024]{1,0:T(2,128)S(1)}, f32[2,1024]{1,0:T(2,128)S(1)}, u32[]{:S(2)}, u32[]{:S(2)}) collective-permute-start(f32[2,1024]{1,0:T(2,128)S(1)} %fusion), channel_id=1, source_target_pairs={{0,2},{2,0},{1,3},{3,1},{4,6},{6,4},{5,7},{7,5},{8,10},{10,8},{9,1... | collective-permute-start | bytes 24584 | tf_op jit(solution)/shard_map/ppermute | solution.py:22

commit v2 on v1

v2 whole, which is shorter than its diff:
```python
import jax
import jax.numpy as jnp
from jax import lax
from jax.experimental import pallas as pl
from jax.experimental.pallas import tpu as pltpu
from jax.sharding import Mesh
from jax.sharding import PartitionSpec as P


DOM = ("xl", "z", "y")
ORB = ("xh", "c")

PEERS = (1, 3, 2)
GROUPS = (3, 2, 3)
EARLY, LATE = GROUPS[0] + GROUPS[1], GROUPS[2]
PAIRS = tuple((l, l) for l in range(4)) + tuple((l, l + 1) for l in range(3)) + tuple((l + 1, l) for l in range(3))
CHUNK = 1024
SMEM = pl.BlockSpec(memory_space=pltpu.SMEM)
VMEM = pl.BlockSpec(memory_space=pltpu.VMEM)


def permute(x, axis, target):
    size = lax.axis_size(axis)
    return lax.ppermute(x, axis, [(i, target(i) % size) for i in range(size)])


def swap(x, axis, distance=1):
    return permute(x, axis, lambda i: i ^ distance)


def pack_kernel(*refs):
    peers = len(PEERS)
    ids, pieces, outs = refs[:peers], refs[peers:-peers], refs[-peers:]
    for g in range(2):
        for n, (source, target) in enumerate(PAIRS):
            for slots, out in zip(ids, outs):
                tile = slots[g, source] * 3 + (target - source + 1)
                for k, piece in enumerate(pieces):
                    for half in range(2):
                        out[g * len(PAIRS) + n, k, half] = piece[half, tile]


def pack(slots, pieces):
    shape = jax.ShapeDtypeStruct((2 * len(PAIRS), len(pieces), *pieces[0].shape[:1], *pieces[0].shape[2:]), pieces[0].dtype)
    return pl.pallas_call(
        pack_kernel,
        out_shape=[shape] * len(slots),
        in_specs=[SMEM] * len(slots) + [VMEM] * len(pieces),
        out_specs=[VMEM] * len(slots),
        compiler_params=pltpu.CompilerParams(vmem_limit_bytes=8 * 2**20),
        cost_estimate=pl.CostEstimate(flops=1000000, bytes_accessed=2000000, transcendentals=0),
    )(*slots, *pieces)


def tile_of(n, g, slots, counts, pattern):
    source, target = PAIRS[n]
    s, t = slots[g, source], slots[g, target]
    column = target - source + 1
    keep = (t - s == target - source) & (pattern[s, column] == 1) & (max(source, target) < counts[g])
    pair = target // 2
    return s * 3 + column, keep, (pair, source - pair, slice(128 * (target % 2), 128 * (target % 2) + 128))


def place(weights, lead, spot, keep, meta, k, parts):
    pair, row, lanes = spot
    my_xl, my_y, my_q, z = meta[0], meta[1], meta[2], meta[3 + k]
    low, high = my_y % 2 == 1, my_y // 2 == 1
    for half, blocks in enumerate(parts):
        quarter = ((my_xl ^ half) * 2 + z // 4) ^ my_q
        start = pl.multiple_of(quarter * 128 + (z % 4) * 32, 32)
        b = [jnp.where(low, blocks[j ^ 1], blocks[j]) for j in range(4)]
        b = [jnp.where(high, b[j ^ 2], b[j]) for j in range(4)]
        group = jnp.concatenate(b, axis=0)
        weights[(*lead, pair, row, pl.ds(start, 32), lanes)] = jnp.where(keep, group, jnp.zeros_like(group))


def parts_of(own, recv, tile, index, k):
    by_distance = dict(zip(PEERS, recv))
    return [
        [own[half, tile]] + [by_distance[j][index, k, half] for j in (1, 2, 3)]
        for half in range(2)
    ]


def assemble_kernel(meta, slots, counts, pattern, *refs):
    own, weights = refs[:EARLY], refs[-1]
    recv = (refs[EARLY : EARLY + 3], refs[EARLY + 3 : EARLY + 6])
    for g in range(2):
        weights[g, 0, 2, :, :128] = jnp.zeros((512, 128), weights.dtype)
        weights[g, 1, 0, :, 128:] = jnp.zeros((512, 128), weights.dtype)
        for n in range(len(PAIRS)):
            tile, keep, spot = tile_of(n, g, slots, counts, pattern)
            for k in range(EARLY):
                part = 0 if k < GROUPS[0] else 1
                parts = parts_of(own[k], recv[part], tile, g * len(PAIRS) + n, k - part * GROUPS[0])
                place(weights, (g,), spot, keep, meta, k, parts)


def assemble(meta, slot_ids, slot_count, pattern, own, recv):
    return pl.pallas_call(
        assemble_kernel,
        out_shape=jax.ShapeDtypeStruct((2, 2, 3, 512, 256), jnp.bfloat16),
        in_specs=[SMEM] * 4 + [VMEM] * (len(own) + len(recv)),
        out_specs=VMEM,
        compiler_params=pltpu.CompilerParams(vmem_limit_bytes=12 * 2**20),
        cost_estimate=pl.CostEstimate(flops=1000000, bytes_accessed=6000000, transcendentals=0),
    )(meta, slot_ids, slot_count, pattern, *own, *recv)


def rotate_kernel(meta, slots, counts, pattern, staged, *refs):
    own, recv, occupation, quarters = refs[:LATE], refs[LATE : LATE + 3], refs[LATE + 3], refs[LATE + 4 : LATE + 8]
    out, density, weights = refs[LATE + 8 :]
    g, p = pl.program_id(0), pl.program_id(1)

    @pl.when(p == 0)
    def _():
        for pair in range(2):
            for row in range(3):
                weights[pair, row] = staged[0, pair, row]
        for n in range(len(PAIRS)):
            tile, keep, spot = tile_of(n, g, slots, counts, pattern)
            for k in range(LATE):
                place(weights, (), spot, keep, meta, EARLY + k, parts_of(own[k], recv, tile, g * len(PAIRS) + n, k))

    total = jnp.zeros((CHUNK, 128), jnp.float32)
    left = [jnp.concatenate([q[0, l] for q in quarters], axis=1) for l in range(4)]
    for pair in range(2):
        acc = None
        for row in range(3):
            part = jnp.dot(left[row + pair], weights[pair, row], preferred_element_type=jnp.float32)
            acc = part if acc is None else acc + part
        rounded = acc.astype(out.dtype)
        for m in range(2):
            mine = rounded[:, 128 * m : 128 * m + 128]
            out[0, 2 * pair + m] = mine
            wide = mine.astype(jnp.float32)
            total = total + wide * wide * occupation[pl.ds(slots[g, 2 * pair + m], 1), :]
    summed = lax.dot_general(
        jnp.ones((8, 128), jnp.float32), total, (((1,), (1,)), ((), ())),
        precision=lax.Precision.HIGHEST, preferred_element_type=jnp.float32,
    )[:1]
    density[pl.ds(g, 1), pl.ds(pl.multiple_of(p * CHUNK, CHUNK), CHUNK)] = summed


def rotate(meta, slot_ids, slot_count, pattern, staged, own, recv, occupation, quarters):
    blocks, slots_per, points, width = quarters[0].shape
    tile = pl.BlockSpec((1, slots_per, CHUNK, width), lambda g, p: (g, 0, p, 0))
    return pl.pallas_call(
        rotate_kernel,
        grid=(blocks, points // CHUNK),
        out_shape=[
            jax.ShapeDtypeStruct(quarters[0].shape, quarters[0].dtype),
            jax.ShapeDtypeStruct((blocks, points), jnp.float32),
        ],
        in_specs=[SMEM] * 4
        + [pl.BlockSpec((1, *staged.shape[1:]), lambda g, p: (g, 0, 0, 0, 0))]
        + [VMEM] * (len(own) + len(recv) + 1)
        + [tile] * 4,
        out_specs=[tile, pl.BlockSpec((blocks, points), lambda g, p: (0, 0))],
        scratch_shapes=[pltpu.VMEM(staged.shape[1:], jnp.bfloat16)],
        compiler_params=pltpu.CompilerParams(
            dimension_semantics=("arbitrary", "arbitrary"), vmem_limit_bytes=32 * 2**20
        ),
        cost_estimate=pl.CostEstimate(flops=3 * 10**9, bytes_accessed=14 * 10**6, transcendentals=0),
    )(meta, slot_ids, slot_count, pattern, staged, *own, *recv, occupation, *quarters)


def body(orbitals, slot_ids, slot_count, band_tiles, pattern, occupation):
    rows = band_tiles.shape[2]
    z, y = lax.axis_index("z"), lax.axis_index("y")
    odd, second_bit = z % 2, z // 2 % 2
    step = jnp.where(odd == 1, -1, 1)
    z_of = [z, z + step, z - step, z ^ 2, jnp.where(second_bit == 1, z + 2, z - 2), z + 3 * step, z - 3 * step, z + 4]
    meta = jnp.stack(
        [lax.axis_index("xl"), y, lax.axis_index("xh") * 2 + lax.axis_index("c")] + [k & 7 for k in z_of]
    ).astype(jnp.int32)
    tiles = band_tiles.reshape(-1, rows, band_tiles.shape[3])
    here = jnp.stack([tiles, swap(tiles, "xl")])
    far_half = swap(orbitals, "xh")
    near_half = swap(orbitals, "c")
    slots = [swap(slot_ids, "y", k) for k in PEERS]

    def even(i):
        return i ^ 1

    def uneven(i):
        return ((i - 1) ^ 1) + 1

    one = [permute(here, "z", even), permute(here, "z", uneven)]
    two = [swap(here, "z", 2), permute(here, "z", lambda i: ((i - 2) ^ 2) + 2)]
    flag = odd != second_bit
    three = [permute(jnp.where(flag, two[0], two[1]), "z", even), permute(jnp.where(flag, two[1], two[0]), "z", uneven)]
    groups = [[here, *one], two, [*three, swap(here, "z", 4)]]
    recv = []
    for blocks in groups:
        packed = pack(slots, blocks)
        recv.append([swap(x, "y", k) for x, k in zip(packed, PEERS)])
    quarters = [orbitals, near_half, far_half, swap(far_half, "c")]
    staged = assemble(meta, slot_ids, slot_count, pattern, groups[0] + groups[1], recv[0] + recv[1])
    rotated, partial = rotate(meta, slot_ids, slot_count, pattern, staged, groups[2], recv[2], occupation, quarters)
    across = swap(partial, "xh")
    diagonal = permute(partial, ("xh", "c"), lambda i: i ^ 3)
    beside = swap(partial, "c")
    return rotated, (partial + beside) + (across + diagonal)


def solution(mesh):
    sizes = (2, 8, 4, 2, 2)
    torus = Mesh(mesh.devices.reshape(sizes), DOM + ORB)
    return jax.shard_map(
        body,
        mesh=torus,
        in_specs=(
            P(DOM, None, None, ORB),
            P(DOM, None),
            P(DOM),
            P(None, None, DOM, ORB),
            P(),
            P(None, ORB),
        ),
        out_specs=(P(DOM, None, None, ORB), P(DOM, None)),
        check_vma=False,
    )
```

time: 160 us -> 152 us (0.950)
  waiting for transfers between devices: 93.9 us -> 72.2 us
  starting transfers between devices: 40 us -> 56.2 us
  Pallas kernels: 17.5 us -> 12.5 us
  local copies, waits for them, and re-layouts: 4.36 us -> 8.54 us
    ppermute x22 -> x26, waiting for transfers between devices: 93.9 us -> 72.2 us  [permute(): return lax.ppermute(x, axis, [(i, target(i) % size) for i in range(size)])]
    ppermute x22 -> x26, starting transfers between devices: 40 us -> 56.2 us  [permute(): return lax.ppermute(x, axis, [(i, target(i) % size) for i in range(size)])]
    pallas_call x1, Pallas kernels: 12.8 us -> 7.57 us  [rotate(): pl.pallas_call(rotate_kernel, grid=(blocks, points // CHUNK), out_shape=[...]
    unnamed x34 -> x39, local copies, waits for them, and re-layouts: 4.36 us -> 8.45 us
    pallas_call x2 -> x4, Pallas kernels: 4.71 us -> 4.95 us  [the longest x3 3.01 us: pack(): pl.pallas_call(pack_kernel, out_shape=[shape] * len(slots), in_specs=[SME...]
  transfers between devices with their start and end apart: 22 -> 26, of which waited for: 13 -> 13; matrix products, arithmetic and copies ran while one was open for 2% -> 1% of each run, Pallas kernels for 3% -> 3%
where the time goes in v2:
time: 152 us
  waiting for transfers between devices  72.2 us (48%)
  starting transfers between devices  56.2 us (37%)
  Pallas kernels  12.5 us (8%)
  local copies, waits for them, and re-layouts  8.54 us (6%)
  other arithmetic  1.55 us (1%)
    ppermute x26, waiting for transfers between devices, permute(): return lax.ppermute(x, axis, [(i, target(i) % size) for i in range(size)])  72.2 us
    ppermute x26, starting transfers between devices, permute(): return lax.ppermute(x, axis, [(i, target(i) % size) for i in range(size)])  56.2 us
    unnamed x39, local copies, waits for them, and re-layouts  8.45 us
    pallas_call x1, Pallas kernels, rotate(): pl.pallas_call(rotate_kernel, grid=(blocks, points // CHUNK), out_shape=[...  7.57 us
  transfers between devices with their start and end apart: 26, of which 13 were waited for; matrix products, arithmetic and copies ran while one was open for 1% of the time, Pallas kernels for 3%

profile of v2, /device:TPU:1, one launch (start us, length us, event | category | flops | bytes accessed | tf_op | source)
XLA Modules:
  0.0 151.8 jit_solution(3013702654389725058)
XLA Ops:
  0.6 0.0 copy-start.16
  0.7 3.6 %collective-permute-start.21 = (bf16[2,4,1024,128]{3,2,1,0:T(8,128)(2,1)}, bf16[2,4,1024,128]{3,2,1,0:T(8,128)(2,1)S(1)}, u32[]{:S(2)}, u32[]{:S(2)}) collective-permute-start(bf16[2,4,1024,128]{3,2,1,0:T(8,128)(2,1)} %refs_7_.1), channel_id=1, source_target_pairs={{0,2},{2,0},{1,3},{3,1},{4,6},{6,4},{5,7},{7,5},{8,10},{10,8},{9,1... | collective-permute-start | bytes 6291464 | tf_op jit(solution)/shard_map/ppermute | solution.py:24
  4.3 1.0 collective-permute-start.20
  5.3 43.7 %collective-permute-done.21.refs_9_ = bf16[2,4,1024,128]{3,2,1,0:T(8,128)(2,1)S(1)} collective-permute-done((bf16[2,4,1024,128]{3,2,1,0:T(8,128)(2,1)}, bf16[2,4,1024,128]{3,2,1,0:T(8,128)(2,1)S(1)}, u32[]{:S(2)}, u32[]{:S(2)}) %collective-permute-start.21) | collective-permute-done | bytes 2097184 | tf_op jit(solution)/shard_map/ppermute | solution.py:24
  48.9 2.2 %collective-permute-start.22 = (bf16[2,4,1024,128]{3,2,1,0:T(8,128)(2,1)S(1)}, bf16[2,4,1024,128]{3,2,1,0:T(8,128)(2,1)}, u32[]{:S(2)}, u32[]{:S(2)}) collective-permute-start(bf16[2,4,1024,128]{3,2,1,0:T(8,128)(2,1)S(1)} %collective-permute-done.21.refs_9_), channel_id=1, source_target_pairs={{0,1},{1,0},{2,3},{3,2},{4,5},{5,4},{6,7},{7,6},{8,9},{9,8},{10,11... | collective-permute-start | bytes 6291464 | tf_op jit(solution)/shard_map/ppermute | solution.py:24
  51.1 1.4 collective-permute-start
  52.5 3.1 %collective-permute-done = bf16[48,8,128]{2,1,0:T(8,128)(2,1)S(1)} collective-permute-done((bf16[48,8,128]{2,1,0:T(8,128)(2,1)}, bf16[48,8,128]{2,1,0:T(8,128)(2,1)S(1)}, u32[]{:S(2)}, u32[]{:S(2)}) %collective-permute-start) | collective-permute-done | bytes 98336 | tf_op jit(solution)/shard_map/ppermute | solution.py:24
  55.7 0.9 pad_maximum_fusion.refs_3_.refs_0_
  56.6 6.3 %collective-permute-start.4 = (bf16[2,48,8,128]{3,2,1,0:T(8,128)(2,1)S(1)}, bf16[2,48,8,128]{3,2,1,0:T(8,128)(2,1)S(1)}, u32[]{:S(2)}, u32[]{:S(2)}) collective-permute-start(bf16[2,48,8,128]{3,2,1,0:T(8,128)(2,1)S(1)} %pad_maximum_fusion.refs_3_.refs_0_), channel_id=1, source_target_pairs={{0,96},{16,112},{32,64},{48,80},{64,32},{80,48},{96,0},{112,16},{1... | collective-permute-start | bytes 589832 | tf_op jit(solution)/shard_map/ppermute | solution.py:24
  62.9 2.9 %collective-permute-start.7 = (s32[2,4]{1,0:T(2,128)}, s32[2,4]{1,0:T(2,128)S(1)}, u32[]{:S(2)}, u32[]{:S(2)}) collective-permute-start(s32[2,4]{1,0:T(2,128)} %slots.3), channel_id=1, source_target_pairs={{0,8},{4,12},{8,0},{12,4},{1,9},{5,13},{9,1},{13,5},{2,10},{6,14},... | collective-permute-start | bytes 104 | tf_op jit(solution)/shard_map/ppermute | solution.py:24
  65.8 0.8 collective-permute-start.6
  66.6 0.7 collective-permute-done.7.refs_2_
  67.3 0.9 collective-permute-start.3
  68.2 1.4 collective-permute-done.6.refs_1_
  69.7 2.6 %collective-permute-done.5.refs_0_ = s32[2,4]{1,0:T(2,128)S(1)} collective-permute-done((s32[2,4]{1,0:T(2,128)}, s32[2,4]{1,0:T(2,128)S(1)}, u32[]{:S(2)}, u32[]{:S(2)}) %collective-permute-start.5) | collective-permute-done | bytes 64 | tf_op jit(solution)/shard_map/ppermute | solution.py:24
  72.3 1.3 collective-permute-start.16
  73.6 2.7 %collective-permute-start.2 = (bf16[2,48,8,128]{3,2,1,0:T(8,128)(2,1)S(1)}, bf16[2,48,8,128]{3,2,1,0:T(8,128)(2,1)S(1)}, u32[]{:S(2)}, u32[]{:S(2)}) collective-permute-start(bf16[2,48,8,128]{3,2,1,0:T(8,128)(2,1)S(1)} %pad_maximum_fusion.refs_3_.refs_0_), channel_id=1, source_target_pairs={{0,112},{16,32},{32,16},{48,64},{64,48},{80,96},{96,80},{112,0},{1... | collective-permute-start | bytes 589832 | tf_op jit(solution)/shard_map/ppermute | solution.py:24
  76.3 0.0 collective-permute-done.3.refs_3_
  76.3 1.3 collective-permute-start.1
  77.6 0.7 shard_map.78
  78.3 5.0 %collective-permute-done.16.refs_5_.refs_2_ = bf16[2,48,8,128]{3,2,1,0:T(8,128)(2,1)S(1)} collective-permute-done((bf16[2,48,8,128]{3,2,1,0:T(8,128)(2,1)S(1)}, bf16[2,48,8,128]{3,2,1,0:T(8,128)(2,1)S(1)}, u32[]{:S(2)}, u32[]{:S(2)}) %collective-permute-start.16) | collective-permute-done | bytes 196640 | tf_op jit(solution)/shard_map/ppermute | solution.py:24
  83.3 3.2 %collective-permute-start.11 = (bf16[20,2,2,8,128]{4,3,2,1,0:T(8,128)(2,1)S(1)}, bf16[20,2,2,8,128]{4,3,2,1,0:T(8,128)(2,1)S(1)}, u32[]{:S(2)}, u32[]{:S(2)}) collective-permute-start(bf16[20,2,2,8,128]{4,3,2,1,0:T(8,128)(2,1)S(1)} %get-tuple-element.16), channel_id=1, source_target_pairs={{0,4},{4,0},{8,12},{12,8},{1,5},{5,1},{9,13},{13,9},{2,6},{6,2},{1... | collective-permute-start | bytes 491528 | tf_op jit(solution)/shard_map/ppermute | solution.py:24
  86.5 0.3 collective-permute-done.2.refs_5_.refs_2_
  86.9 1.5 collective-permute-start.12
  88.4 0.0 collective-permute-done.1.refs_4_.refs_1_
  88.4 1.3 collective-permute-start.15
  89.7 0.0 collective-permute-done.11.refs_8_
  89.7 4.7 %collective-permute-start.14 = (bf16[2,48,8,128]{3,2,1,0:T(8,128)(2,1)S(1)}, bf16[2,48,8,128]{3,2,1,0:T(8,128)(2,1)S(1)}, u32[]{:S(2)}, u32[]{:S(2)}) collective-permute-start(bf16[2,48,8,128]{3,2,1,0:T(8,128)(2,1)S(1)} %get-tuple-element.25), channel_id=1, source_target_pairs={{0,16},{16,0},{32,48},{48,32},{64,80},{80,64},{96,112},{112,96},{1... | collective-permute-start | bytes 589832 | tf_op jit(solution)/shard_map/ppermute | solution.py:24
  94.4 0.4 collective-permute-start.13
  94.7 0.7 shard_map.77
  95.5 4.7 %collective-permute-done.13.refs_10_ = bf16[20,2,2,8,128]{4,3,2,1,0:T(8,128)(2,1)S(1)} collective-permute-done((bf16[20,2,2,8,128]{4,3,2,1,0:T(8,128)(2,1)S(1)}, bf16[20,2,2,8,128]{4,3,2,1,0:T(8,128)(2,1)S(1)}, u32[]{:S(2)}, u32[]{:S(2)}) %collective-permute-start.13) | collective-permute-done | bytes 163872 | tf_op jit(solution)/shard_map/ppermute | solution.py:24
  100.2 0.0 collective-permute-start.8
  100.2 0.0 collective-permute-done.15.refs_4_.refs_1_
  100.2 0.6 collective-permute-start.9
  100.8 0.0 collective-permute-done.14.refs_3_.refs_0_
  100.8 2.6 %collective-permute-start.10 = (bf16[20,3,2,8,128]{4,3,2,1,0:T(8,128)(2,1)S(1)}, bf16[20,3,2,8,128]{4,3,2,1,0:T(8,128)(2,1)S(1)}, u32[]{:S(2)}, u32[]{:S(2)}) collective-permute-start(bf16[20,3,2,8,128]{4,3,2,1,0:T(8,128)(2,1)S(1)} %get-tuple-element.15), channel_id=1, source_target_pairs={{0,8},{4,12},{8,0},{12,4},{1,9},{5,13},{9,1},{13,5},{2,10},{6,14},... | collective-permute-start | bytes 737288 | tf_op jit(solution)/shard_map/ppermute | solution.py:24
  103.4 1.6 %shard_map.80 = (bf16[20,3,2,8,128]{4,3,2,1,0:T(8,128)(2,1)}, bf16[20,3,2,8,128]{4,3,2,1,0:T(8,128)(2,1)}, bf16[20,3,2,8,128]{4,3,2,1,0:T(8,128)(2,1)}) custom-call(s32[2,4]{1,0:T(2,128)S(1)} %collective-permute-done.5.refs_0_, s32[2,4]{1,0:T(2,128)S(1)} %collective-permute-done.6.refs_1_, s32[2,4]{1,0:T(2,128)S(1)} %collective-permute-done.7.refs_2_, ...), custom_call_target="tpu_custom_call" | custom-call | flops 1000000 | bytes 2000000 | tf_op jit(solution)/shard_map/pallas_call | solution.py:45
  105.0 0.7 copy-done.1
  105.7 0.5 collective-permute-done.8.refs_5_
  106.2 0.7 copy-done.3
  106.9 0.0 collective-permute-start.17
  106.9 4.0 %collective-permute-done.9.refs_6_ = bf16[20,3,2,8,128]{4,3,2,1,0:T(8,128)(2,1)S(1)} collective-permute-done((bf16[20,3,2,8,128]{4,3,2,1,0:T(8,128)(2,1)S(1)}, bf16[20,3,2,8,128]{4,3,2,1,0:T(8,128)(2,1)S(1)}, u32[]{:S(2)}, u32[]{:S(2)}) %collective-permute-start.9) | collective-permute-done | bytes 245792 | tf_op jit(solution)/shard_map/ppermute | solution.py:24
  110.9 0.7 copy-done.5
  111.6 0.0 collective-permute-start.18
  111.6 0.7 copy-done.7
  112.3 1.9 %collective-permute-start.19 = (bf16[20,3,2,8,128]{4,3,2,1,0:T(8,128)(2,1)}, bf16[20,3,2,8,128]{4,3,2,1,0:T(8,128)(2,1)}, u32[]{:S(2)}, u32[]{:S(2)}) collective-permute-start(bf16[20,3,2,8,128]{4,3,2,1,0:T(8,128)(2,1)} %get-tuple-element.21), channel_id=1, source_target_pairs={{0,8},{4,12},{8,0},{12,4},{1,9},{5,13},{9,1},{13,5},{2,10},{6,14},... | collective-permute-start | bytes 737288 | tf_op jit(solution)/shard_map/ppermute | solution.py:24
  114.3 0.1 copy.9.pattern
  114.4 0.1 stack.53.meta
  114.5 0.0 copy-start.4
  114.5 0.9 copy-done.4
  115.4 0.9 copy-done.6
  116.4 0.9 copy-done.8
  117.3 0.9 copy-done.10
  118.2 0.9 copy-done.12
  119.1 0.9 copy-done.14
  120.0 1.9 %shard_map.79.staged = bf16[2,2,3,512,256]{4,3,2,1,0:T(8,128)(2,1)S(1)} custom-call(s32[11]{0:T(128)S(1)} %stack.53.meta, s32[2,4]{1,0:T(2,128)S(1)} %copy-done.16, s32[2]{0:T(128)S(1)} %copy-done.17, s32[16,3]{1,0:T(8,128)S(1)} %copy.9.pattern, bf16[2,48,8,128]{3,2,1,0:T(8,128)(2,1)S(1)} %pad_maximum_fusion.refs_3_.refs_0_, ...), custom_call_target="tpu_custom_call" | custom-call | flops 1000000 | bytes 6000000 | tf_op jit(solution)/shard_map/pallas_call | solution.py:100
  122.0 2.5 %collective-permute-done.18.refs_4_ = bf16[20,3,2,8,128]{4,3,2,1,0:T(8,128)(2,1)} collective-permute-done((bf16[20,3,2,8,128]{4,3,2,1,0:T(8,128)(2,1)}, bf16[20,3,2,8,128]{4,3,2,1,0:T(8,128)(2,1)}, u32[]{:S(2)}, u32[]{:S(2)}) %collective-permute-start.18) | collective-permute-done | bytes 245792 | tf_op jit(solution)/shard_map/ppermute | solution.py:24
  124.5 7.6 %shard_map.81 = (bf16[2,4,1024,128]{3,2,1,0:T(8,128)(2,1)}, f32[2,1024]{1,0:T(2,128)S(1)}) custom-call(s32[11]{0:T(128)S(1)} %stack.53.meta, s32[2,4]{1,0:T(2,128)S(1)} %copy-done.16, s32[2]{0:T(128)S(1)} %copy-done.17, s32[16,3]{1,0:T(8,128)S(1)} %copy.9.pattern, bf16[2,2,3,512,256]{4,3,2,1,0:T(8,128)(2,1)S(1)} %shard_map.79.staged, ...), custom_call_target="tpu_custom_call" | custom-call | flops 3000000000 | bytes 14000000 | tf_op jit(solution)/shard_map/pallas_call | solution.py:148
  132.1 15.1 %collective-permute-start.25 = (f32[2,1024]{1,0:T(2,128)S(1)}, f32[2,1024]{1,0:T(2,128)S(1)}, u32[]{:S(2)}, u32[]{:S(2)}) collective-permute-start(f32[2,1024]{1,0:T(2,128)S(1)} %get-tuple-element.23), channel_id=1, source_target_pairs={{0,3},{1,2},{2,1},{3,0},{4,7},{5,6},{6,5},{7,4},{8,11},{9,10},{10,... | collective-permute-start | bytes 24584 | tf_op jit(solution)/shard_map/ppermute | solution.py:24
  147.2 0.2 collective-permute-start.24
  147.4 0.3 collective-permute-start.23
  147.7 1.1 collective-permute-done.25
  148.8 2.4 %collective-permute-done.24 = f32[2,1024]{1,0:T(2,128)S(1)} collective-permute-done((f32[2,1024]{1,0:T(2,128)S(1)}, f32[2,1024]{1,0:T(2,128)S(1)}, u32[]{:S(2)}, u32[]{:S(2)}) %collective-permute-start.24) | collective-permute-done | bytes 8224 | tf_op jit(solution)/shard_map/ppermute | solution.py:24
  151.2 0.6 add_add_fusion
  (36 shorter events, 0.1 us)
Async XLA Ops:
  0.6 113.8 %copy-start.16 = (s32[2,4]{1,0:T(2,128)S(1)}, s32[2,4]{1,0:T(2,128)}, u32[]{:S(2)}) copy-start(s32[2,4]{1,0:T(2,128)} %slots.3) | copy-start | bytes 100
  0.6 113.6 %copy-start.18 = (s32[16,3]{0,1:T(4,128)S(1)}, s32[16,3]{0,1:T(4,128)}, u32[]{:S(2)}) copy-start(s32[16,3]{0,1:T(4,128)} %param.10) | copy-start | bytes 580
  0.7 113.8 %copy-start.17 = (s32[2]{0:T(128)S(1)}, s32[2]{0:T(128)}, u32[]{:S(2)}) copy-start(s32[2]{0:T(128)} %counts.3) | copy-start | bytes 28
  0.7 48.3 %collective-permute-start.21 = (bf16[2,4,1024,128]{3,2,1,0:T(8,128)(2,1)}, bf16[2,4,1024,128]{3,2,1,0:T(8,128)(2,1)S(1)}, u32[]{:S(2)}, u32[]{:S(2)}) collective-permute-start(bf16[2,4,1024,128]{3,2,1,0:T(8,128)(2,1)} %refs_7_.1), channel_id=1, source_target_pairs={{0,2},{2,0},{1,3},{3,1},{4,6},{6,4},{5,7},{7,5},{8,10},{10,8},{9,1... | collective-permute-start | bytes 6291464 | tf_op jit(solution)/shard_map/ppermute | solution.py:24
  4.3 120.2 %collective-permute-start.20 = (bf16[2,4,1024,128]{3,2,1,0:T(8,128)(2,1)}, bf16[2,4,1024,128]{3,2,1,0:T(8,128)(2,1)}, u32[]{:S(2)}, u32[]{:S(2)}) collective-permute-start(bf16[2,4,1024,128]{3,2,1,0:T(8,128)(2,1)} %refs_7_.1), channel_id=1, source_target_pairs={{0,1},{1,0},{2,3},{3,2},{4,5},{5,4},{6,7},{7,6},{8,9},{9,8},{10,11... | collective-permute-start | bytes 6291464 | tf_op jit(solution)/shard_map/ppermute | solution.py:24
  48.9 75.5 %collective-permute-start.22 = (bf16[2,4,1024,128]{3,2,1,0:T(8,128)(2,1)S(1)}, bf16[2,4,1024,128]{3,2,1,0:T(8,128)(2,1)}, u32[]{:S(2)}, u32[]{:S(2)}) collective-permute-start(bf16[2,4,1024,128]{3,2,1,0:T(8,128)(2,1)S(1)} %collective-permute-done.21.refs_9_), channel_id=1, source_target_pairs={{0,1},{1,0},{2,3},{3,2},{4,5},{5,4},{6,7},{7,6},{8,9},{9,8},{10,11... | collective-permute-start | bytes 6291464 | tf_op jit(solution)/shard_map/ppermute | solution.py:24
  51.1 4.6 %collective-permute-start = (bf16[48,8,128]{2,1,0:T(8,128)(2,1)}, bf16[48,8,128]{2,1,0:T(8,128)(2,1)S(1)}, u32[]{:S(2)}, u32[]{:S(2)}) collective-permute-start(bf16[48,8,128]{2,1,0:T(8,128)(2,1)} %bitcast.14), channel_id=1, source_target_pairs={{0,128},{128,0},{1,129},{129,1},{2,130},{130,2},{3,131},{131,3},{4... | collective-permute-start | bytes 294920 | tf_op jit(solution)/shard_map/ppermute | solution.py:24
  56.6 17.0 %collective-permute-start.4 = (bf16[2,48,8,128]{3,2,1,0:T(8,128)(2,1)S(1)}, bf16[2,48,8,128]{3,2,1,0:T(8,128)(2,1)S(1)}, u32[]{:S(2)}, u32[]{:S(2)}) collective-permute-start(bf16[2,48,8,128]{3,2,1,0:T(8,128)(2,1)S(1)} %pad_maximum_fusion.refs_3_.refs_0_), channel_id=1, source_target_pairs={{0,96},{16,112},{32,64},{48,80},{64,32},{80,48},{96,0},{112,16},{1... | collective-permute-start | bytes 589832 | tf_op jit(solution)/shard_map/ppermute | solution.py:24
  62.9 4.4 %collective-permute-start.7 = (s32[2,4]{1,0:T(2,128)}, s32[2,4]{1,0:T(2,128)S(1)}, u32[]{:S(2)}, u32[]{:S(2)}) collective-permute-start(s32[2,4]{1,0:T(2,128)} %slots.3), channel_id=1, source_target_pairs={{0,8},{4,12},{8,0},{12,4},{1,9},{5,13},{9,1},{13,5},{2,10},{6,14},... | collective-permute-start | bytes 104 | tf_op jit(solution)/shard_map/ppermute | solution.py:24
  65.8 3.8 %collective-permute-start.6 = (s32[2,4]{1,0:T(2,128)}, s32[2,4]{1,0:T(2,128)S(1)}, u32[]{:S(2)}, u32[]{:S(2)}) collective-permute-start(s32[2,4]{1,0:T(2,128)} %slots.3), channel_id=1, source_target_pairs={{0,12},{4,8},{8,4},{12,0},{1,13},{5,9},{9,5},{13,1},{2,14},{6,10},... | collective-permute-start | bytes 104 | tf_op jit(solution)/shard_map/ppermute | solution.py:24
  67.3 9.0 %collective-permute-start.3 = (bf16[2,48,8,128]{3,2,1,0:T(8,128)(2,1)S(1)}, bf16[2,48,8,128]{3,2,1,0:T(8,128)(2,1)S(1)}, u32[]{:S(2)}, u32[]{:S(2)}) collective-permute-start(bf16[2,48,8,128]{3,2,1,0:T(8,128)(2,1)S(1)} %pad_maximum_fusion.refs_3_.refs_0_), channel_id=1, source_target_pairs={{0,32},{16,48},{32,0},{48,16},{64,96},{80,112},{96,64},{112,80},{1... | collective-permute-start | bytes 589832 | tf_op jit(solution)/shard_map/ppermute | solution.py:24
  69.7 2.6 %collective-permute-start.5 = (s32[2,4]{1,0:T(2,128)}, s32[2,4]{1,0:T(2,128)S(1)}, u32[]{:S(2)}, u32[]{:S(2)}) collective-permute-start(s32[2,4]{1,0:T(2,128)} %slots.3), channel_id=1, source_target_pairs={{0,4},{4,0},{8,12},{12,8},{1,5},{5,1},{9,13},{13,9},{2,6},{6,2},{1... | collective-permute-start | bytes 104 | tf_op jit(solution)/shard_map/ppermute | solution.py:24
  72.3 11.0 %collective-permute-start.16 = (bf16[2,48,8,128]{3,2,1,0:T(8,128)(2,1)S(1)}, bf16[2,48,8,128]{3,2,1,0:T(8,128)(2,1)S(1)}, u32[]{:S(2)}, u32[]{:S(2)}) collective-permute-start(bf16[2,48,8,128]{3,2,1,0:T(8,128)(2,1)S(1)} %pad_maximum_fusion.refs_3_.refs_0_), channel_id=1, source_target_pairs={{0,64},{16,80},{32,96},{48,112},{64,0},{80,16},{96,32},{112,48},{1... | collective-permute-start | bytes 589832 | tf_op jit(solution)/shard_map/ppermute | solution.py:24
  73.6 13.3 %collective-permute-start.2 = (bf16[2,48,8,128]{3,2,1,0:T(8,128)(2,1)S(1)}, bf16[2,48,8,128]{3,2,1,0:T(8,128)(2,1)S(1)}, u32[]{:S(2)}, u32[]{:S(2)}) collective-permute-start(bf16[2,48,8,128]{3,2,1,0:T(8,128)(2,1)S(1)} %pad_maximum_fusion.refs_3_.refs_0_), channel_id=1, source_target_pairs={{0,112},{16,32},{32,16},{48,64},{64,48},{80,96},{96,80},{112,0},{1... | collective-permute-start | bytes 589832 | tf_op jit(solution)/shard_map/ppermute | solution.py:24
  76.3 12.0 %collective-permute-start.1 = (bf16[2,48,8,128]{3,2,1,0:T(8,128)(2,1)S(1)}, bf16[2,48,8,128]{3,2,1,0:T(8,128)(2,1)S(1)}, u32[]{:S(2)}, u32[]{:S(2)}) collective-permute-start(bf16[2,48,8,128]{3,2,1,0:T(8,128)(2,1)S(1)} %pad_maximum_fusion.refs_3_.refs_0_), channel_id=1, source_target_pairs={{0,16},{16,0},{32,48},{48,32},{64,80},{80,64},{96,112},{112,96},{1... | collective-permute-start | bytes 589832 | tf_op jit(solution)/shard_map/ppermute | solution.py:24
  83.3 6.4 %collective-permute-start.11 = (bf16[20,2,2,8,128]{4,3,2,1,0:T(8,128)(2,1)S(1)}, bf16[20,2,2,8,128]{4,3,2,1,0:T(8,128)(2,1)S(1)}, u32[]{:S(2)}, u32[]{:S(2)}) collective-permute-start(bf16[20,2,2,8,128]{4,3,2,1,0:T(8,128)(2,1)S(1)} %get-tuple-element.16), channel_id=1, source_target_pairs={{0,4},{4,0},{8,12},{12,8},{1,5},{5,1},{9,13},{13,9},{2,6},{6,2},{1... | collective-permute-start | bytes 491528 | tf_op jit(solution)/shard_map/ppermute | solution.py:24
  86.9 7.5 %collective-permute-start.12 = (bf16[20,2,2,8,128]{4,3,2,1,0:T(8,128)(2,1)S(1)}, bf16[20,2,2,8,128]{4,3,2,1,0:T(8,128)(2,1)S(1)}, u32[]{:S(2)}, u32[]{:S(2)}) collective-permute-start(bf16[20,2,2,8,128]{4,3,2,1,0:T(8,128)(2,1)S(1)} %get-tuple-element.17), channel_id=1, source_target_pairs={{0,12},{4,8},{8,4},{12,0},{1,13},{5,9},{9,5},{13,1},{2,14},{6,10},... | collective-permute-start | bytes 491528 | tf_op jit(solution)/shard_map/ppermute | solution.py:24
  88.4 11.8 %collective-permute-start.15 = (bf16[2,48,8,128]{3,2,1,0:T(8,128)(2,1)S(1)}, bf16[2,48,8,128]{3,2,1,0:T(8,128)(2,1)S(1)}, u32[]{:S(2)}, u32[]{:S(2)}) collective-permute-start(bf16[2,48,8,128]{3,2,1,0:T(8,128)(2,1)S(1)} %get-tuple-element.24), channel_id=1, source_target_pairs={{0,112},{16,32},{32,16},{48,64},{64,48},{80,96},{96,80},{112,0},{1... | collective-permute-start | bytes 589832 | tf_op jit(solution)/shard_map/ppermute | solution.py:24
  89.7 21.9 %copy-start.9 = (bf16[20,2,2,8,128]{4,3,2,1,0:T(8,128)(2,1)}, bf16[20,2,2,8,128]{4,3,2,1,0:T(8,128)(2,1)S(1)}, u32[]{:S(2)}) copy-start(bf16[20,2,2,8,128]{4,3,2,1,0:T(8,128)(2,1)S(1)} %collective-permute-done.11.refs_8_) | copy-start | bytes 491524
  89.7 11.1 %collective-permute-start.14 = (bf16[2,48,8,128]{3,2,1,0:T(8,128)(2,1)S(1)}, bf16[2,48,8,128]{3,2,1,0:T(8,128)(2,1)S(1)}, u32[]{:S(2)}, u32[]{:S(2)}) collective-permute-start(bf16[2,48,8,128]{3,2,1,0:T(8,128)(2,1)S(1)} %get-tuple-element.25), channel_id=1, source_target_pairs={{0,16},{16,0},{32,48},{48,32},{64,80},{80,64},{96,112},{112,96},{1... | collective-permute-start | bytes 589832 | tf_op jit(solution)/shard_map/ppermute | solution.py:24
  94.4 17.9 %copy-start.11 = (bf16[20,2,2,8,128]{4,3,2,1,0:T(8,128)(2,1)}, bf16[20,2,2,8,128]{4,3,2,1,0:T(8,128)(2,1)S(1)}, u32[]{:S(2)}) copy-start(bf16[20,2,2,8,128]{4,3,2,1,0:T(8,128)(2,1)S(1)} %collective-permute-done.12.refs_9_) | copy-start | bytes 491524
  94.4 5.8 %collective-permute-start.13 = (bf16[20,2,2,8,128]{4,3,2,1,0:T(8,128)(2,1)S(1)}, bf16[20,2,2,8,128]{4,3,2,1,0:T(8,128)(2,1)S(1)}, u32[]{:S(2)}, u32[]{:S(2)}) collective-permute-start(bf16[20,2,2,8,128]{4,3,2,1,0:T(8,128)(2,1)S(1)} %get-tuple-element.18), channel_id=1, source_target_pairs={{0,8},{4,12},{8,0},{12,4},{1,9},{5,13},{9,1},{13,5},{2,10},{6,14},... | collective-permute-start | bytes 491528 | tf_op jit(solution)/shard_map/ppermute | solution.py:24
  100.2 12.2 %copy-start.13 = (bf16[20,2,2,8,128]{4,3,2,1,0:T(8,128)(2,1)}, bf16[20,2,2,8,128]{4,3,2,1,0:T(8,128)(2,1)S(1)}, u32[]{:S(2)}) copy-start(bf16[20,2,2,8,128]{4,3,2,1,0:T(8,128)(2,1)S(1)} %collective-permute-done.13.refs_10_) | copy-start | bytes 491524
  100.2 6.1 %collective-permute-start.8 = (bf16[20,3,2,8,128]{4,3,2,1,0:T(8,128)(2,1)S(1)}, bf16[20,3,2,8,128]{4,3,2,1,0:T(8,128)(2,1)S(1)}, u32[]{:S(2)}, u32[]{:S(2)}) collective-permute-start(bf16[20,3,2,8,128]{4,3,2,1,0:T(8,128)(2,1)S(1)} %get-tuple-element.13), channel_id=1, source_target_pairs={{0,4},{4,0},{8,12},{12,8},{1,5},{5,1},{9,13},{13,9},{2,6},{6,2},{1... | collective-permute-start | bytes 737288 | tf_op jit(solution)/shard_map/ppermute | solution.py:24
  100.2 10.7 %collective-permute-start.9 = (bf16[20,3,2,8,128]{4,3,2,1,0:T(8,128)(2,1)S(1)}, bf16[20,3,2,8,128]{4,3,2,1,0:T(8,128)(2,1)S(1)}, u32[]{:S(2)}, u32[]{:S(2)}) collective-permute-start(bf16[20,3,2,8,128]{4,3,2,1,0:T(8,128)(2,1)S(1)} %get-tuple-element.14), channel_id=1, source_target_pairs={{0,12},{4,8},{8,4},{12,0},{1,13},{5,9},{9,5},{13,1},{2,14},{6,10},... | collective-permute-start | bytes 737288 | tf_op jit(solution)/shard_map/ppermute | solution.py:24
  100.8 10.8 %collective-permute-start.10 = (bf16[20,3,2,8,128]{4,3,2,1,0:T(8,128)(2,1)S(1)}, bf16[20,3,2,8,128]{4,3,2,1,0:T(8,128)(2,1)S(1)}, u32[]{:S(2)}, u32[]{:S(2)}) collective-permute-start(bf16[20,3,2,8,128]{4,3,2,1,0:T(8,128)(2,1)S(1)} %get-tuple-element.15), channel_id=1, source_target_pairs={{0,8},{4,12},{8,0},{12,4},{1,9},{5,13},{9,1},{13,5},{2,10},{6,14},... | collective-permute-start | bytes 737288 | tf_op jit(solution)/shard_map/ppermute | solution.py:24
  105.0 0.7 copy-start.1
  106.2 0.7 copy-start.3
  106.9 15.1 %collective-permute-start.17 = (bf16[20,3,2,8,128]{4,3,2,1,0:T(8,128)(2,1)}, bf16[20,3,2,8,128]{4,3,2,1,0:T(8,128)(2,1)}, u32[]{:S(2)}, u32[]{:S(2)}) collective-permute-start(bf16[20,3,2,8,128]{4,3,2,1,0:T(8,128)(2,1)} %get-tuple-element.19), channel_id=1, source_target_pairs={{0,4},{4,0},{8,12},{12,8},{1,5},{5,1},{9,13},{13,9},{2,6},{6,2},{1... | collective-permute-start | bytes 737288 | tf_op jit(solution)/shard_map/ppermute | solution.py:24
  110.9 0.7 copy-start.5
  111.6 12.9 %collective-permute-start.18 = (bf16[20,3,2,8,128]{4,3,2,1,0:T(8,128)(2,1)}, bf16[20,3,2,8,128]{4,3,2,1,0:T(8,128)(2,1)}, u32[]{:S(2)}, u32[]{:S(2)}) collective-permute-start(bf16[20,3,2,8,128]{4,3,2,1,0:T(8,128)(2,1)} %get-tuple-element.20), channel_id=1, source_target_pairs={{0,12},{4,8},{8,4},{12,0},{1,13},{5,9},{9,5},{13,1},{2,14},{6,10},... | collective-permute-start | bytes 737288 | tf_op jit(solution)/shard_map/ppermute | solution.py:24
  111.6 0.7 copy-start.7
  112.3 12.2 %collective-permute-start.19 = (bf16[20,3,2,8,128]{4,3,2,1,0:T(8,128)(2,1)}, bf16[20,3,2,8,128]{4,3,2,1,0:T(8,128)(2,1)}, u32[]{:S(2)}, u32[]{:S(2)}) collective-permute-start(bf16[20,3,2,8,128]{4,3,2,1,0:T(8,128)(2,1)} %get-tuple-element.21), channel_id=1, source_target_pairs={{0,8},{4,12},{8,0},{12,4},{1,9},{5,13},{9,1},{13,5},{2,10},{6,14},... | collective-permute-start | bytes 737288 | tf_op jit(solution)/shard_map/ppermute | solution.py:24
  114.5 0.9 copy-start.4
  115.4 0.9 copy-start.6
  116.3 0.9 copy-start.8
  117.3 0.9 copy-start.10
  118.2 0.9 copy-start.12
  119.1 0.9 copy-start.14
  120.0 4.5 %copy-start = (bf16[2,4,1024,128]{3,2,1,0:T(8,128)(2,1)S(1)}, bf16[2,4,1024,128]{3,2,1,0:T(8,128)(2,1)}, u32[]{:S(2)}) copy-start(bf16[2,4,1024,128]{3,2,1,0:T(8,128)(2,1)} %refs_7_.1) | copy-start | bytes 6291460
  120.0 4.5 %copy-start.2 = (bf16[2,48,8,128]{3,2,1,0:T(8,128)(2,1)S(1)}, bf16[2,48,8,128]{3,2,1,0:T(8,128)(2,1)}, u32[]{:S(2)}) copy-start(bf16[2,48,8,128]{3,2,1,0:T(8,128)(2,1)} %copy-done.1) | copy-start | bytes 589828
  120.0 4.5 %copy-start.15 = (f32[16,128]{1,0:T(8,128)S(1)}, f32[16,128]{1,0:T(8,128)}, u32[]{:S(2)}) copy-start(f32[16,128]{1,0:T(8,128)} %refs_6_.1) | copy-start | bytes 24580
  132.1 16.7 %collective-permute-start.25 = (f32[2,1024]{1,0:T(2,128)S(1)}, f32[2,1024]{1,0:T(2,128)S(1)}, u32[]{:S(2)}, u32[]{:S(2)}) collective-permute-start(f32[2,1024]{1,0:T(2,128)S(1)} %get-tuple-element.23), channel_id=1, source_target_pairs={{0,3},{1,2},{2,1},{3,0},{4,7},{5,6},{6,5},{7,4},{8,11},{9,10},{10,... | collective-permute-start | bytes 24584 | tf_op jit(solution)/shard_map/ppermute | solution.py:24
  147.2 4.0 %collective-permute-start.24 = (f32[2,1024]{1,0:T(2,128)S(1)}, f32[2,1024]{1,0:T(2,128)S(1)}, u32[]{:S(2)}, u32[]{:S(2)}) collective-permute-start(f32[2,1024]{1,0:T(2,128)S(1)} %get-tuple-element.23), channel_id=1, source_target_pairs={{0,2},{2,0},{1,3},{3,1},{4,6},{6,4},{5,7},{7,5},{8,10},{10,8},{9,1... | collective-permute-start | bytes 24584 | tf_op jit(solution)/shard_map/ppermute | solution.py:24
  147.4 3.8 %collective-permute-start.23 = (f32[2,1024]{1,0:T(2,128)S(1)}, f32[2,1024]{1,0:T(2,128)S(1)}, u32[]{:S(2)}, u32[]{:S(2)}) collective-permute-start(f32[2,1024]{1,0:T(2,128)S(1)} %get-tuple-element.23), channel_id=1, source_target_pairs={{0,1},{1,0},{2,3},{3,2},{4,5},{5,4},{6,7},{7,6},{8,9},{9,8},{10,11... | collective-permute-start | bytes 24584 | tf_op jit(solution)/shard_map/ppermute | solution.py:24

commit v3 on v2

--- a/solution.py
+++ b/solution.py
@@ -67,11 +67,11 @@
     low, high = my_y % 2 == 1, my_y // 2 == 1
     for half, blocks in enumerate(parts):
         quarter = ((my_xl ^ half) * 2 + z // 4) ^ my_q
-        start = pl.multiple_of(quarter * 128 + (z % 4) * 32, 32)
+        start = pl.multiple_of(row * 512 + quarter * 128 + (z % 4) * 32, 32)
         b = [jnp.where(low, blocks[j ^ 1], blocks[j]) for j in range(4)]
         b = [jnp.where(high, b[j ^ 2], b[j]) for j in range(4)]
         group = jnp.concatenate(b, axis=0)
-        weights[(*lead, pair, row, pl.ds(start, 32), lanes)] = jnp.where(keep, group, jnp.zeros_like(group))
+        weights[(*lead, pair, pl.ds(start, 32), lanes)] = jnp.where(keep, group, jnp.zeros_like(group))
 
 
 def parts_of(own, recv, tile, index, k):
@@ -86,8 +86,8 @@
     own, weights = refs[:EARLY], refs[-1]
     recv = (refs[EARLY : EARLY + 3], refs[EARLY + 3 : EARLY + 6])
     for g in range(2):
-        weights[g, 0, 2, :, :128] = jnp.zeros((512, 128), weights.dtype)
-        weights[g, 1, 0, :, 128:] = jnp.zeros((512, 128), weights.dtype)
+        weights[g, 0, 1024:, :128] = jnp.zeros((512, 128), weights.dtype)
+        weights[g, 1, :512, 128:] = jnp.zeros((512, 128), weights.dtype)
         for n in range(len(PAIRS)):
             tile, keep, spot = tile_of(n, g, slots, counts, pattern)
             for k in range(EARLY):
@@ -99,7 +99,7 @@
 def assemble(meta, slot_ids, slot_count, pattern, own, recv):
     return pl.pallas_call(
         assemble_kernel,
-        out_shape=jax.ShapeDtypeStruct((2, 2, 3, 512, 256), jnp.bfloat16),
+        out_shape=jax.ShapeDtypeStruct((2, 2, 1536, 256), jnp.bfloat16),
         in_specs=[SMEM] * 4 + [VMEM] * (len(own) + len(recv)),
         out_specs=VMEM,
         compiler_params=pltpu.CompilerParams(vmem_limit_bytes=12 * 2**20),
@@ -115,20 +115,16 @@
     @pl.when(p == 0)
     def _():
         for pair in range(2):
-            for row in range(3):
-                weights[pair, row] = staged[0, pair, row]
+            weights[pair] = staged[0, pair]
         for n in range(len(PAIRS)):
             tile, keep, spot = tile_of(n, g, slots, counts, pattern)
             for k in range(LATE):
                 place(weights, (), spot, keep, meta, EARLY + k, parts_of(own[k], recv, tile, g * len(PAIRS) + n, k))
 
     total = jnp.zeros((CHUNK, 128), jnp.float32)
-    left = [jnp.concatenate([q[0, l] for q in quarters], axis=1) for l in range(4)]
     for pair in range(2):
-        acc = None
-        for row in range(3):
-            part = jnp.dot(left[row + pair], weights[pair, row], preferred_element_type=jnp.float32)
-            acc = part if acc is None else acc + part
+        left = jnp.concatenate([q[0, pair + row] for row in range(3) for q in quarters], axis=1)
+        acc = jnp.dot(left, weights[pair], preferred_element_type=jnp.float32)
         rounded = acc.astype(out.dtype)
         for m in range(2):
             mine = rounded[:, 128 * m : 128 * m + 128]
@@ -153,7 +149,7 @@
             jax.ShapeDtypeStruct((blocks, points), jnp.float32),
         ],
         in_specs=[SMEM] * 4
-        + [pl.BlockSpec((1, *staged.shape[1:]), lambda g, p: (g, 0, 0, 0, 0))]
+        + [pl.BlockSpec((1, *staged.shape[1:]), lambda g, p: (g, 0, 0, 0))]
         + [VMEM] * (len(own) + len(recv) + 1)
         + [tile] * 4,
         out_specs=[tile, pl.BlockSpec((blocks, points), lambda g, p: (0, 0))],
@@ -190,7 +186,7 @@
     two = [swap(here, "z", 2), permute(here, "z", lambda i: ((i - 2) ^ 2) + 2)]
     flag = odd != second_bit
     three = [permute(jnp.where(flag, two[0], two[1]), "z", even), permute(jnp.where(flag, two[1], two[0]), "z", uneven)]
-    groups = [[here, *one], two, [*three, swap(here, "z", 4)]]
+    groups = [[here, *one], two, [*three, swap(two[1], "z", 2)]]
     recv = []
     for blocks in groups:
         packed = pack(slots, blocks)

time: 152 us -> 142 us (0.934)
  starting transfers between devices: 56.2 us -> 48 us
  waiting for transfers between devices: 72.2 us -> 70.5 us
    ppermute x26, starting transfers between devices: 56.2 us -> 48 us  [permute(): return lax.ppermute(x, axis, [(i, target(i) % size) for i in range(size)])]
    ppermute x26, waiting for transfers between devices: 72.2 us -> 70.5 us  [permute(): return lax.ppermute(x, axis, [(i, target(i) % size) for i in range(size)])]
  transfers between devices with their start and end apart: 26 -> 26, of which waited for: 13 -> 15; matrix products, arithmetic and copies ran while one was open for 1% -> 1% of each run, Pallas kernels for 3% -> 4%
where the time goes in v3:
time: 142 us
  waiting for transfers between devices  70.5 us (50%)
  starting transfers between devices  48 us (34%)
  Pallas kernels  12.7 us (9%)
  local copies, waits for them, and re-layouts  8.55 us (6%)
  other arithmetic  1.55 us (1%)
    ppermute x26, waiting for transfers between devices, permute(): return lax.ppermute(x, axis, [(i, target(i) % size) for i in range(size)])  70.5 us
    ppermute x26, starting transfers between devices, permute(): return lax.ppermute(x, axis, [(i, target(i) % size) for i in range(size)])  48 us
    unnamed x39, local copies, waits for them, and re-layouts  8.46 us
    pallas_call x1, Pallas kernels, rotate(): pl.pallas_call(rotate_kernel, grid=(blocks, points // CHUNK), out_shape=[...  7.64 us
    pallas_call x3, Pallas kernels, pack(): pl.pallas_call(pack_kernel, out_shape=[shape] * len(slots), in_specs=[SME...  3.02 us
  transfers between devices with their start and end apart: 26, of which 15 were waited for; matrix products, arithmetic and copies ran while one was open for 1% of the time, Pallas kernels for 4%

profile of v3, /device:TPU:1, one launch (start us, length us, event | category | flops | bytes accessed | tf_op | source)
XLA Modules:
  0.0 142.1 jit_solution(949913718324404239)
XLA Ops:
  0.6 0.0 copy-start.16
  0.7 3.6 %collective-permute-start.21 = (bf16[2,4,1024,128]{3,2,1,0:T(8,128)(2,1)}, bf16[2,4,1024,128]{3,2,1,0:T(8,128)(2,1)S(1)}, u32[]{:S(2)}, u32[]{:S(2)}) collective-permute-start(bf16[2,4,1024,128]{3,2,1,0:T(8,128)(2,1)} %refs_7_.1), channel_id=1, source_target_pairs={{0,2},{2,0},{1,3},{3,1},{4,6},{6,4},{5,7},{7,5},{8,10},{10,8},{9,1... | collective-permute-start | bytes 6291464 | tf_op jit(solution)/shard_map/ppermute | solution.py:24
  4.3 1.0 collective-permute-start.20
  5.3 43.7 %collective-permute-done.21.refs_9_ = bf16[2,4,1024,128]{3,2,1,0:T(8,128)(2,1)S(1)} collective-permute-done((bf16[2,4,1024,128]{3,2,1,0:T(8,128)(2,1)}, bf16[2,4,1024,128]{3,2,1,0:T(8,128)(2,1)S(1)}, u32[]{:S(2)}, u32[]{:S(2)}) %collective-permute-start.21) | collective-permute-done | bytes 2097184 | tf_op jit(solution)/shard_map/ppermute | solution.py:24
  48.9 2.2 %collective-permute-start.22 = (bf16[2,4,1024,128]{3,2,1,0:T(8,128)(2,1)S(1)}, bf16[2,4,1024,128]{3,2,1,0:T(8,128)(2,1)}, u32[]{:S(2)}, u32[]{:S(2)}) collective-permute-start(bf16[2,4,1024,128]{3,2,1,0:T(8,128)(2,1)S(1)} %collective-permute-done.21.refs_9_), channel_id=1, source_target_pairs={{0,1},{1,0},{2,3},{3,2},{4,5},{5,4},{6,7},{7,6},{8,9},{9,8},{10,11... | collective-permute-start | bytes 6291464 | tf_op jit(solution)/shard_map/ppermute | solution.py:24
  51.1 1.4 %collective-permute-start = (bf16[48,8,128]{2,1,0:T(8,128)(2,1)}, bf16[48,8,128]{2,1,0:T(8,128)(2,1)S(1)}, u32[]{:S(2)}, u32[]{:S(2)}) collective-permute-start(bf16[48,8,128]{2,1,0:T(8,128)(2,1)} %bitcast.14), channel_id=1, source_target_pairs={{0,128},{128,0},{1,129},{129,1},{2,130},{130,2},{3,131},{131,3},{4... | collective-permute-start | bytes 294920 | tf_op jit(solution)/shard_map/ppermute | solution.py:24
  52.5 3.1 %collective-permute-done = bf16[48,8,128]{2,1,0:T(8,128)(2,1)S(1)} collective-permute-done((bf16[48,8,128]{2,1,0:T(8,128)(2,1)}, bf16[48,8,128]{2,1,0:T(8,128)(2,1)S(1)}, u32[]{:S(2)}, u32[]{:S(2)}) %collective-permute-start) | collective-permute-done | bytes 98336 | tf_op jit(solution)/shard_map/ppermute | solution.py:24
  55.7 0.9 pad_maximum_fusion.refs_3_.refs_0_
  56.6 6.3 %collective-permute-start.4 = (bf16[2,48,8,128]{3,2,1,0:T(8,128)(2,1)S(1)}, bf16[2,48,8,128]{3,2,1,0:T(8,128)(2,1)S(1)}, u32[]{:S(2)}, u32[]{:S(2)}) collective-permute-start(bf16[2,48,8,128]{3,2,1,0:T(8,128)(2,1)S(1)} %pad_maximum_fusion.refs_3_.refs_0_), channel_id=1, source_target_pairs={{0,96},{16,112},{32,64},{48,80},{64,32},{80,48},{96,0},{112,16},{1... | collective-permute-start | bytes 589832 | tf_op jit(solution)/shard_map/ppermute | solution.py:24
  62.9 2.9 %collective-permute-start.7 = (s32[2,4]{1,0:T(2,128)}, s32[2,4]{1,0:T(2,128)S(1)}, u32[]{:S(2)}, u32[]{:S(2)}) collective-permute-start(s32[2,4]{1,0:T(2,128)} %slots.3), channel_id=1, source_target_pairs={{0,8},{4,12},{8,0},{12,4},{1,9},{5,13},{9,1},{13,5},{2,10},{6,14},... | collective-permute-start | bytes 104 | tf_op jit(solution)/shard_map/ppermute | solution.py:24
  65.8 1.2 collective-permute-start.3
  67.0 0.3 collective-permute-done.7.refs_2_
  67.3 2.7 %collective-permute-start.6 = (s32[2,4]{1,0:T(2,128)}, s32[2,4]{1,0:T(2,128)S(1)}, u32[]{:S(2)}, u32[]{:S(2)}) collective-permute-start(s32[2,4]{1,0:T(2,128)} %slots.3), channel_id=1, source_target_pairs={{0,12},{4,8},{8,4},{12,0},{1,13},{5,9},{9,5},{13,1},{2,14},{6,10},... | collective-permute-start | bytes 104 | tf_op jit(solution)/shard_map/ppermute | solution.py:24
  70.1 1.3 collective-permute-done.6.refs_1_
  71.4 2.9 %collective-permute-done.5.refs_0_ = s32[2,4]{1,0:T(2,128)S(1)} collective-permute-done((s32[2,4]{1,0:T(2,128)}, s32[2,4]{1,0:T(2,128)S(1)}, u32[]{:S(2)}, u32[]{:S(2)}) %collective-permute-start.5) | collective-permute-done | bytes 64 | tf_op jit(solution)/shard_map/ppermute | solution.py:24
  74.3 0.0 collective-permute-start.2
  74.3 1.3 collective-permute-start.1
  75.6 0.7 shard_map.78
  76.3 0.1 collective-permute-start.11
  76.4 3.6 %collective-permute-done.2.refs_5_.refs_2_ = bf16[2,48,8,128]{3,2,1,0:T(8,128)(2,1)S(1)} collective-permute-done((bf16[2,48,8,128]{3,2,1,0:T(8,128)(2,1)S(1)}, bf16[2,48,8,128]{3,2,1,0:T(8,128)(2,1)S(1)}, u32[]{:S(2)}, u32[]{:S(2)}) %collective-permute-start.2) | collective-permute-done | bytes 196640 | tf_op jit(solution)/shard_map/ppermute | solution.py:24
  80.1 2.7 %collective-permute-start.12 = (bf16[20,2,2,8,128]{4,3,2,1,0:T(8,128)(2,1)S(1)}, bf16[20,2,2,8,128]{4,3,2,1,0:T(8,128)(2,1)S(1)}, u32[]{:S(2)}, u32[]{:S(2)}) collective-permute-start(bf16[20,2,2,8,128]{4,3,2,1,0:T(8,128)(2,1)S(1)} %get-tuple-element.17), channel_id=1, source_target_pairs={{0,12},{4,8},{8,4},{12,0},{1,13},{5,9},{9,5},{13,1},{2,14},{6,10},... | collective-permute-start | bytes 491528 | tf_op jit(solution)/shard_map/ppermute | solution.py:24
  82.7 0.0 collective-permute-done.1.refs_4_.refs_1_
  82.7 0.0 collective-permute-start.13
  82.8 0.0 collective-permute-done.11.refs_8_
  82.8 0.8 collective-permute-start.16
  83.6 2.7 %collective-permute-done.12.refs_9_ = bf16[20,2,2,8,128]{4,3,2,1,0:T(8,128)(2,1)S(1)} collective-permute-done((bf16[20,2,2,8,128]{4,3,2,1,0:T(8,128)(2,1)S(1)}, bf16[20,2,2,8,128]{4,3,2,1,0:T(8,128)(2,1)S(1)}, u32[]{:S(2)}, u32[]{:S(2)}) %collective-permute-start.12) | collective-permute-done | bytes 163872 | tf_op jit(solution)/shard_map/ppermute | solution.py:24
  86.3 0.0 collective-permute-start.15
  86.3 3.6 %collective-permute-done.13.refs_10_ = bf16[20,2,2,8,128]{4,3,2,1,0:T(8,128)(2,1)S(1)} collective-permute-done((bf16[20,2,2,8,128]{4,3,2,1,0:T(8,128)(2,1)S(1)}, bf16[20,2,2,8,128]{4,3,2,1,0:T(8,128)(2,1)S(1)}, u32[]{:S(2)}, u32[]{:S(2)}) %collective-permute-start.13) | collective-permute-done | bytes 163872 | tf_op jit(solution)/shard_map/ppermute | solution.py:24
  89.9 0.7 shard_map.77
  90.6 0.0 collective-permute-done.16.refs_5_.refs_2_
  90.6 0.2 collective-permute-start.8
  90.8 1.2 collective-permute-done.15.refs_4_.refs_1_
  92.0 3.7 %collective-permute-start.9 = (bf16[20,3,2,8,128]{4,3,2,1,0:T(8,128)(2,1)S(1)}, bf16[20,3,2,8,128]{4,3,2,1,0:T(8,128)(2,1)S(1)}, u32[]{:S(2)}, u32[]{:S(2)}) collective-permute-start(bf16[20,3,2,8,128]{4,3,2,1,0:T(8,128)(2,1)S(1)} %get-tuple-element.14), channel_id=1, source_target_pairs={{0,12},{4,8},{8,4},{12,0},{1,13},{5,9},{9,5},{13,1},{2,14},{6,10},... | collective-permute-start | bytes 737288 | tf_op jit(solution)/shard_map/ppermute | solution.py:24
  95.7 0.9 collective-permute-done.14.refs_3_.refs_0_
  96.7 0.0 collective-permute-start.10
  96.7 1.6 %shard_map.80 = (bf16[20,3,2,8,128]{4,3,2,1,0:T(8,128)(2,1)}, bf16[20,3,2,8,128]{4,3,2,1,0:T(8,128)(2,1)}, bf16[20,3,2,8,128]{4,3,2,1,0:T(8,128)(2,1)}) custom-call(s32[2,4]{1,0:T(2,128)S(1)} %collective-permute-done.5.refs_0_, s32[2,4]{1,0:T(2,128)S(1)} %collective-permute-done.6.refs_1_, s32[2,4]{1,0:T(2,128)S(1)} %collective-permute-done.7.refs_2_, ...), custom_call_target="tpu_custom_call" | custom-call | flops 1000000 | bytes 2000000 | tf_op jit(solution)/shard_map/pallas_call | solution.py:45
  98.3 0.7 copy-done.1
  98.9 0.0 collective-permute-done.8.refs_5_
  98.9 0.7 copy-done.3
  99.6 0.0 collective-permute-start.17
  99.6 1.9 %collective-permute-done.9.refs_6_ = bf16[20,3,2,8,128]{4,3,2,1,0:T(8,128)(2,1)S(1)} collective-permute-done((bf16[20,3,2,8,128]{4,3,2,1,0:T(8,128)(2,1)S(1)}, bf16[20,3,2,8,128]{4,3,2,1,0:T(8,128)(2,1)S(1)}, u32[]{:S(2)}, u32[]{:S(2)}) %collective-permute-start.9) | collective-permute-done | bytes 245792 | tf_op jit(solution)/shard_map/ppermute | solution.py:24
  101.5 0.7 copy-done.5
  102.2 3.1 %collective-permute-start.18 = (bf16[20,3,2,8,128]{4,3,2,1,0:T(8,128)(2,1)}, bf16[20,3,2,8,128]{4,3,2,1,0:T(8,128)(2,1)}, u32[]{:S(2)}, u32[]{:S(2)}) collective-permute-start(bf16[20,3,2,8,128]{4,3,2,1,0:T(8,128)(2,1)} %get-tuple-element.20), channel_id=1, source_target_pairs={{0,12},{4,8},{8,4},{12,0},{1,13},{5,9},{9,5},{13,1},{2,14},{6,10},... | collective-permute-start | bytes 737288 | tf_op jit(solution)/shard_map/ppermute | solution.py:24
  105.3 0.7 copy-done.7
  106.0 0.0 collective-permute-start.19
  106.1 0.1 copy.9.pattern
  106.2 0.1 stack.53.meta
  106.3 0.0 copy-start.4
  106.3 0.9 copy-done.4
  107.2 0.9 copy-done.6
  108.2 0.9 copy-done.8
  109.1 0.9 copy-done.10
  110.0 0.9 copy-done.12
  111.0 0.9 copy-done.14
  111.9 2.0 %shard_map.79.staged = bf16[2,2,1536,256]{3,2,1,0:T(8,128)(2,1)S(1)} custom-call(s32[11]{0:T(128)S(1)} %stack.53.meta, s32[2,4]{1,0:T(2,128)S(1)} %copy-done.16, s32[2]{0:T(128)S(1)} %copy-done.17, s32[16,3]{1,0:T(8,128)S(1)} %copy.9.pattern, bf16[2,48,8,128]{3,2,1,0:T(8,128)(2,1)S(1)} %pad_maximum_fusion.refs_3_.refs_0_, ...), custom_call_target="tpu_custom_call" | custom-call | flops 1000000 | bytes 6000000 | tf_op jit(solution)/shard_map/pallas_call | solution.py:100
  113.9 0.8 collective-permute-done.18.refs_4_
  114.6 0.9 collective-permute-done.19.refs_5_
  115.6 7.6 %shard_map.81 = (bf16[2,4,1024,128]{3,2,1,0:T(8,128)(2,1)}, f32[2,1024]{1,0:T(2,128)S(1)}) custom-call(s32[11]{0:T(128)S(1)} %stack.53.meta, s32[2,4]{1,0:T(2,128)S(1)} %copy-done.16, s32[2]{0:T(128)S(1)} %copy-done.17, s32[16,3]{1,0:T(8,128)S(1)} %copy.9.pattern, bf16[2,2,1536,256]{3,2,1,0:T(8,128)(2,1)S(1)} %shard_map.79.staged, ...), custom_call_target="tpu_custom_call" | custom-call | flops 3000000000 | bytes 14000000 | tf_op jit(solution)/shard_map/pallas_call | solution.py:144
  123.3 14.2 %collective-permute-start.25 = (f32[2,1024]{1,0:T(2,128)S(1)}, f32[2,1024]{1,0:T(2,128)S(1)}, u32[]{:S(2)}, u32[]{:S(2)}) collective-permute-start(f32[2,1024]{1,0:T(2,128)S(1)} %get-tuple-element.23), channel_id=1, source_target_pairs={{0,3},{1,2},{2,1},{3,0},{4,7},{5,6},{6,5},{7,4},{8,11},{9,10},{10,... | collective-permute-start | bytes 24584 | tf_op jit(solution)/shard_map/ppermute | solution.py:24
  137.5 0.2 collective-permute-start.24
  137.7 0.3 collective-permute-start.23
  138.0 1.1 collective-permute-done.25
  139.0 2.4 %collective-permute-done.24 = f32[2,1024]{1,0:T(2,128)S(1)} collective-permute-done((f32[2,1024]{1,0:T(2,128)S(1)}, f32[2,1024]{1,0:T(2,128)S(1)}, u32[]{:S(2)}, u32[]{:S(2)}) %collective-permute-start.24) | collective-permute-done | bytes 8224 | tf_op jit(solution)/shard_map/ppermute | solution.py:24
  141.5 0.6 add_add_fusion
  (36 shorter events, 0.1 us)
Async XLA Ops:
  0.6 105.6 %copy-start.16 = (s32[2,4]{1,0:T(2,128)S(1)}, s32[2,4]{1,0:T(2,128)}, u32[]{:S(2)}) copy-start(s32[2,4]{1,0:T(2,128)} %slots.3) | copy-start | bytes 100
  0.6 105.5 %copy-start.18 = (s32[16,3]{0,1:T(4,128)S(1)}, s32[16,3]{0,1:T(4,128)}, u32[]{:S(2)}) copy-start(s32[16,3]{0,1:T(4,128)} %param.10) | copy-start | bytes 580
  0.7 105.6 %copy-start.17 = (s32[2]{0:T(128)S(1)}, s32[2]{0:T(128)}, u32[]{:S(2)}) copy-start(s32[2]{0:T(128)} %counts.3) | copy-start | bytes 28
  0.7 48.3 %collective-permute-start.21 = (bf16[2,4,1024,128]{3,2,1,0:T(8,128)(2,1)}, bf16[2,4,1024,128]{3,2,1,0:T(8,128)(2,1)S(1)}, u32[]{:S(2)}, u32[]{:S(2)}) collective-permute-start(bf16[2,4,1024,128]{3,2,1,0:T(8,128)(2,1)} %refs_7_.1), channel_id=1, source_target_pairs={{0,2},{2,0},{1,3},{3,1},{4,6},{6,4},{5,7},{7,5},{8,10},{10,8},{9,1... | collective-permute-start | bytes 6291464 | tf_op jit(solution)/shard_map/ppermute | solution.py:24
  4.3 111.3 %collective-permute-start.20 = (bf16[2,4,1024,128]{3,2,1,0:T(8,128)(2,1)}, bf16[2,4,1024,128]{3,2,1,0:T(8,128)(2,1)}, u32[]{:S(2)}, u32[]{:S(2)}) collective-permute-start(bf16[2,4,1024,128]{3,2,1,0:T(8,128)(2,1)} %refs_7_.1), channel_id=1, source_target_pairs={{0,1},{1,0},{2,3},{3,2},{4,5},{5,4},{6,7},{7,6},{8,9},{9,8},{10,11... | collective-permute-start | bytes 6291464 | tf_op jit(solution)/shard_map/ppermute | solution.py:24
  48.9 66.7 %collective-permute-start.22 = (bf16[2,4,1024,128]{3,2,1,0:T(8,128)(2,1)S(1)}, bf16[2,4,1024,128]{3,2,1,0:T(8,128)(2,1)}, u32[]{:S(2)}, u32[]{:S(2)}) collective-permute-start(bf16[2,4,1024,128]{3,2,1,0:T(8,128)(2,1)S(1)} %collective-permute-done.21.refs_9_), channel_id=1, source_target_pairs={{0,1},{1,0},{2,3},{3,2},{4,5},{5,4},{6,7},{7,6},{8,9},{9,8},{10,11... | collective-permute-start | bytes 6291464 | tf_op jit(solution)/shard_map/ppermute | solution.py:24
  51.1 4.6 %collective-permute-start = (bf16[48,8,128]{2,1,0:T(8,128)(2,1)}, bf16[48,8,128]{2,1,0:T(8,128)(2,1)S(1)}, u32[]{:S(2)}, u32[]{:S(2)}) collective-permute-start(bf16[48,8,128]{2,1,0:T(8,128)(2,1)} %bitcast.14), channel_id=1, source_target_pairs={{0,128},{128,0},{1,129},{129,1},{2,130},{130,2},{3,131},{131,3},{4... | collective-permute-start | bytes 294920 | tf_op jit(solution)/shard_map/ppermute | solution.py:24
  56.6 17.7 %collective-permute-start.4 = (bf16[2,48,8,128]{3,2,1,0:T(8,128)(2,1)S(1)}, bf16[2,48,8,128]{3,2,1,0:T(8,128)(2,1)S(1)}, u32[]{:S(2)}, u32[]{:S(2)}) collective-permute-start(bf16[2,48,8,128]{3,2,1,0:T(8,128)(2,1)S(1)} %pad_maximum_fusion.refs_3_.refs_0_), channel_id=1, source_target_pairs={{0,96},{16,112},{32,64},{48,80},{64,32},{80,48},{96,0},{112,16},{1... | collective-permute-start | bytes 589832 | tf_op jit(solution)/shard_map/ppermute | solution.py:24
  62.9 4.4 %collective-permute-start.7 = (s32[2,4]{1,0:T(2,128)}, s32[2,4]{1,0:T(2,128)S(1)}, u32[]{:S(2)}, u32[]{:S(2)}) collective-permute-start(s32[2,4]{1,0:T(2,128)} %slots.3), channel_id=1, source_target_pairs={{0,8},{4,12},{8,0},{12,4},{1,9},{5,13},{9,1},{13,5},{2,10},{6,14},... | collective-permute-start | bytes 104 | tf_op jit(solution)/shard_map/ppermute | solution.py:24
  65.8 9.8 %collective-permute-start.3 = (bf16[2,48,8,128]{3,2,1,0:T(8,128)(2,1)S(1)}, bf16[2,48,8,128]{3,2,1,0:T(8,128)(2,1)S(1)}, u32[]{:S(2)}, u32[]{:S(2)}) collective-permute-start(bf16[2,48,8,128]{3,2,1,0:T(8,128)(2,1)S(1)} %pad_maximum_fusion.refs_3_.refs_0_), channel_id=1, source_target_pairs={{0,32},{16,48},{32,0},{48,16},{64,96},{80,112},{96,64},{112,80},{1... | collective-permute-start | bytes 589832 | tf_op jit(solution)/shard_map/ppermute | solution.py:24
  67.3 4.0 %collective-permute-start.6 = (s32[2,4]{1,0:T(2,128)}, s32[2,4]{1,0:T(2,128)S(1)}, u32[]{:S(2)}, u32[]{:S(2)}) collective-permute-start(s32[2,4]{1,0:T(2,128)} %slots.3), channel_id=1, source_target_pairs={{0,12},{4,8},{8,4},{12,0},{1,13},{5,9},{9,5},{13,1},{2,14},{6,10},... | collective-permute-start | bytes 104 | tf_op jit(solution)/shard_map/ppermute | solution.py:24
  71.4 2.9 %collective-permute-start.5 = (s32[2,4]{1,0:T(2,128)}, s32[2,4]{1,0:T(2,128)S(1)}, u32[]{:S(2)}, u32[]{:S(2)}) collective-permute-start(s32[2,4]{1,0:T(2,128)} %slots.3), channel_id=1, source_target_pairs={{0,4},{4,0},{8,12},{12,8},{1,5},{5,1},{9,13},{13,9},{2,6},{6,2},{1... | collective-permute-start | bytes 104 | tf_op jit(solution)/shard_map/ppermute | solution.py:24
  74.3 5.7 %collective-permute-start.2 = (bf16[2,48,8,128]{3,2,1,0:T(8,128)(2,1)S(1)}, bf16[2,48,8,128]{3,2,1,0:T(8,128)(2,1)S(1)}, u32[]{:S(2)}, u32[]{:S(2)}) collective-permute-start(bf16[2,48,8,128]{3,2,1,0:T(8,128)(2,1)S(1)} %pad_maximum_fusion.refs_3_.refs_0_), channel_id=1, source_target_pairs={{0,112},{16,32},{32,16},{48,64},{64,48},{80,96},{96,80},{112,0},{1... | collective-permute-start | bytes 589832 | tf_op jit(solution)/shard_map/ppermute | solution.py:24
  74.3 8.4 %collective-permute-start.1 = (bf16[2,48,8,128]{3,2,1,0:T(8,128)(2,1)S(1)}, bf16[2,48,8,128]{3,2,1,0:T(8,128)(2,1)S(1)}, u32[]{:S(2)}, u32[]{:S(2)}) collective-permute-start(bf16[2,48,8,128]{3,2,1,0:T(8,128)(2,1)S(1)} %pad_maximum_fusion.refs_3_.refs_0_), channel_id=1, source_target_pairs={{0,16},{16,0},{32,48},{48,32},{64,80},{80,64},{96,112},{112,96},{1... | collective-permute-start | bytes 589832 | tf_op jit(solution)/shard_map/ppermute | solution.py:24
  76.3 6.4 %collective-permute-start.11 = (bf16[20,2,2,8,128]{4,3,2,1,0:T(8,128)(2,1)S(1)}, bf16[20,2,2,8,128]{4,3,2,1,0:T(8,128)(2,1)S(1)}, u32[]{:S(2)}, u32[]{:S(2)}) collective-permute-start(bf16[20,2,2,8,128]{4,3,2,1,0:T(8,128)(2,1)S(1)} %get-tuple-element.16), channel_id=1, source_target_pairs={{0,4},{4,0},{8,12},{12,8},{1,5},{5,1},{9,13},{13,9},{2,6},{6,2},{1... | collective-permute-start | bytes 491528 | tf_op jit(solution)/shard_map/ppermute | solution.py:24
  80.1 6.2 %collective-permute-start.12 = (bf16[20,2,2,8,128]{4,3,2,1,0:T(8,128)(2,1)S(1)}, bf16[20,2,2,8,128]{4,3,2,1,0:T(8,128)(2,1)S(1)}, u32[]{:S(2)}, u32[]{:S(2)}) collective-permute-start(bf16[20,2,2,8,128]{4,3,2,1,0:T(8,128)(2,1)S(1)} %get-tuple-element.17), channel_id=1, source_target_pairs={{0,12},{4,8},{8,4},{12,0},{1,13},{5,9},{9,5},{13,1},{2,14},{6,10},... | collective-permute-start | bytes 491528 | tf_op jit(solution)/shard_map/ppermute | solution.py:24
  82.7 7.1 %collective-permute-start.13 = (bf16[20,2,2,8,128]{4,3,2,1,0:T(8,128)(2,1)S(1)}, bf16[20,2,2,8,128]{4,3,2,1,0:T(8,128)(2,1)S(1)}, u32[]{:S(2)}, u32[]{:S(2)}) collective-permute-start(bf16[20,2,2,8,128]{4,3,2,1,0:T(8,128)(2,1)S(1)} %get-tuple-element.18), channel_id=1, source_target_pairs={{0,8},{4,12},{8,0},{12,4},{1,9},{5,13},{9,1},{13,5},{2,10},{6,14},... | collective-permute-start | bytes 491528 | tf_op jit(solution)/shard_map/ppermute | solution.py:24
  82.8 22.6 %copy-start.9 = (bf16[20,2,2,8,128]{4,3,2,1,0:T(8,128)(2,1)}, bf16[20,2,2,8,128]{4,3,2,1,0:T(8,128)(2,1)S(1)}, u32[]{:S(2)}) copy-start(bf16[20,2,2,8,128]{4,3,2,1,0:T(8,128)(2,1)S(1)} %collective-permute-done.11.refs_8_) | copy-start | bytes 491524
  82.8 7.8 %collective-permute-start.16 = (bf16[2,48,8,128]{3,2,1,0:T(8,128)(2,1)S(1)}, bf16[2,48,8,128]{3,2,1,0:T(8,128)(2,1)S(1)}, u32[]{:S(2)}, u32[]{:S(2)}) collective-permute-start(bf16[2,48,8,128]{3,2,1,0:T(8,128)(2,1)S(1)} %collective-permute-done.4.refs_4_), channel_id=1, source_target_pairs={{0,32},{16,48},{32,0},{48,16},{64,96},{80,112},{96,64},{112,80},{1... | collective-permute-start | bytes 589832 | tf_op jit(solution)/shard_map/ppermute | solution.py:24
  86.3 19.7 %copy-start.11 = (bf16[20,2,2,8,128]{4,3,2,1,0:T(8,128)(2,1)}, bf16[20,2,2,8,128]{4,3,2,1,0:T(8,128)(2,1)S(1)}, u32[]{:S(2)}) copy-start(bf16[20,2,2,8,128]{4,3,2,1,0:T(8,128)(2,1)S(1)} %collective-permute-done.12.refs_9_) | copy-start | bytes 491524
  86.3 5.7 %collective-permute-start.15 = (bf16[2,48,8,128]{3,2,1,0:T(8,128)(2,1)S(1)}, bf16[2,48,8,128]{3,2,1,0:T(8,128)(2,1)S(1)}, u32[]{:S(2)}, u32[]{:S(2)}) collective-permute-start(bf16[2,48,8,128]{3,2,1,0:T(8,128)(2,1)S(1)} %get-tuple-element.24), channel_id=1, source_target_pairs={{0,112},{16,32},{32,16},{48,64},{64,48},{80,96},{96,80},{112,0},{1... | collective-permute-start | bytes 589832 | tf_op jit(solution)/shard_map/ppermute | solution.py:24
  89.9 16.2 %copy-start.13 = (bf16[20,2,2,8,128]{4,3,2,1,0:T(8,128)(2,1)}, bf16[20,2,2,8,128]{4,3,2,1,0:T(8,128)(2,1)S(1)}, u32[]{:S(2)}) copy-start(bf16[20,2,2,8,128]{4,3,2,1,0:T(8,128)(2,1)S(1)} %collective-permute-done.13.refs_10_) | copy-start | bytes 491524
  89.9 6.8 %collective-permute-start.14 = (bf16[2,48,8,128]{3,2,1,0:T(8,128)(2,1)S(1)}, bf16[2,48,8,128]{3,2,1,0:T(8,128)(2,1)S(1)}, u32[]{:S(2)}, u32[]{:S(2)}) collective-permute-start(bf16[2,48,8,128]{3,2,1,0:T(8,128)(2,1)S(1)} %get-tuple-element.25), channel_id=1, source_target_pairs={{0,16},{16,0},{32,48},{48,32},{64,80},{80,64},{96,112},{112,96},{1... | collective-permute-start | bytes 589832 | tf_op jit(solution)/shard_map/ppermute | solution.py:24
  90.6 8.3 %collective-permute-start.8 = (bf16[20,3,2,8,128]{4,3,2,1,0:T(8,128)(2,1)S(1)}, bf16[20,3,2,8,128]{4,3,2,1,0:T(8,128)(2,1)S(1)}, u32[]{:S(2)}, u32[]{:S(2)}) collective-permute-start(bf16[20,3,2,8,128]{4,3,2,1,0:T(8,128)(2,1)S(1)} %get-tuple-element.13), channel_id=1, source_target_pairs={{0,4},{4,0},{8,12},{12,8},{1,5},{5,1},{9,13},{13,9},{2,6},{6,2},{1... | collective-permute-start | bytes 737288 | tf_op jit(solution)/shard_map/ppermute | solution.py:24
  92.0 9.5 %collective-permute-start.9 = (bf16[20,3,2,8,128]{4,3,2,1,0:T(8,128)(2,1)S(1)}, bf16[20,3,2,8,128]{4,3,2,1,0:T(8,128)(2,1)S(1)}, u32[]{:S(2)}, u32[]{:S(2)}) collective-permute-start(bf16[20,3,2,8,128]{4,3,2,1,0:T(8,128)(2,1)S(1)} %get-tuple-element.14), channel_id=1, source_target_pairs={{0,12},{4,8},{8,4},{12,0},{1,13},{5,9},{9,5},{13,1},{2,14},{6,10},... | collective-permute-start | bytes 737288 | tf_op jit(solution)/shard_map/ppermute | solution.py:24
  96.7 8.7 %collective-permute-start.10 = (bf16[20,3,2,8,128]{4,3,2,1,0:T(8,128)(2,1)S(1)}, bf16[20,3,2,8,128]{4,3,2,1,0:T(8,128)(2,1)S(1)}, u32[]{:S(2)}, u32[]{:S(2)}) collective-permute-start(bf16[20,3,2,8,128]{4,3,2,1,0:T(8,128)(2,1)S(1)} %get-tuple-element.15), channel_id=1, source_target_pairs={{0,8},{4,12},{8,0},{12,4},{1,9},{5,13},{9,1},{13,5},{2,10},{6,14},... | collective-permute-start | bytes 737288 | tf_op jit(solution)/shard_map/ppermute | solution.py:24
  98.3 0.7 copy-start.1
  98.9 0.7 copy-start.3
  99.6 14.3 %collective-permute-start.17 = (bf16[20,3,2,8,128]{4,3,2,1,0:T(8,128)(2,1)}, bf16[20,3,2,8,128]{4,3,2,1,0:T(8,128)(2,1)}, u32[]{:S(2)}, u32[]{:S(2)}) collective-permute-start(bf16[20,3,2,8,128]{4,3,2,1,0:T(8,128)(2,1)} %get-tuple-element.19), channel_id=1, source_target_pairs={{0,4},{4,0},{8,12},{12,8},{1,5},{5,1},{9,13},{13,9},{2,6},{6,2},{1... | collective-permute-start | bytes 737288 | tf_op jit(solution)/shard_map/ppermute | solution.py:24
  101.5 0.7 copy-start.5
  102.2 12.4 %collective-permute-start.18 = (bf16[20,3,2,8,128]{4,3,2,1,0:T(8,128)(2,1)}, bf16[20,3,2,8,128]{4,3,2,1,0:T(8,128)(2,1)}, u32[]{:S(2)}, u32[]{:S(2)}) collective-permute-start(bf16[20,3,2,8,128]{4,3,2,1,0:T(8,128)(2,1)} %get-tuple-element.20), channel_id=1, source_target_pairs={{0,12},{4,8},{8,4},{12,0},{1,13},{5,9},{9,5},{13,1},{2,14},{6,10},... | collective-permute-start | bytes 737288 | tf_op jit(solution)/shard_map/ppermute | solution.py:24
  105.3 0.7 copy-start.7
  106.0 9.5 %collective-permute-start.19 = (bf16[20,3,2,8,128]{4,3,2,1,0:T(8,128)(2,1)}, bf16[20,3,2,8,128]{4,3,2,1,0:T(8,128)(2,1)}, u32[]{:S(2)}, u32[]{:S(2)}) collective-permute-start(bf16[20,3,2,8,128]{4,3,2,1,0:T(8,128)(2,1)} %get-tuple-element.21), channel_id=1, source_target_pairs={{0,8},{4,12},{8,0},{12,4},{1,9},{5,13},{9,1},{13,5},{2,10},{6,14},... | collective-permute-start | bytes 737288 | tf_op jit(solution)/shard_map/ppermute | solution.py:24
  106.3 0.9 copy-start.4
  107.2 0.9 copy-start.6
  108.2 0.9 copy-start.8
  109.1 0.9 copy-start.10
  110.0 0.9 copy-start.12
  111.0 0.9 copy-start.14
  111.9 3.7 %copy-start = (bf16[2,4,1024,128]{3,2,1,0:T(8,128)(2,1)S(1)}, bf16[2,4,1024,128]{3,2,1,0:T(8,128)(2,1)}, u32[]{:S(2)}) copy-start(bf16[2,4,1024,128]{3,2,1,0:T(8,128)(2,1)} %refs_7_.1) | copy-start | bytes 6291460
  111.9 3.7 %copy-start.2 = (bf16[2,48,8,128]{3,2,1,0:T(8,128)(2,1)S(1)}, bf16[2,48,8,128]{3,2,1,0:T(8,128)(2,1)}, u32[]{:S(2)}) copy-start(bf16[2,48,8,128]{3,2,1,0:T(8,128)(2,1)} %copy-done.1) | copy-start | bytes 589828
  111.9 3.7 %copy-start.15 = (f32[16,128]{1,0:T(8,128)S(1)}, f32[16,128]{1,0:T(8,128)}, u32[]{:S(2)}) copy-start(f32[16,128]{1,0:T(8,128)} %refs_6_.1) | copy-start | bytes 24580
  123.3 15.8 %collective-permute-start.25 = (f32[2,1024]{1,0:T(2,128)S(1)}, f32[2,1024]{1,0:T(2,128)S(1)}, u32[]{:S(2)}, u32[]{:S(2)}) collective-permute-start(f32[2,1024]{1,0:T(2,128)S(1)} %get-tuple-element.23), channel_id=1, source_target_pairs={{0,3},{1,2},{2,1},{3,0},{4,7},{5,6},{6,5},{7,4},{8,11},{9,10},{10,... | collective-permute-start | bytes 24584 | tf_op jit(solution)/shard_map/ppermute | solution.py:24
  137.5 4.0 %collective-permute-start.24 = (f32[2,1024]{1,0:T(2,128)S(1)}, f32[2,1024]{1,0:T(2,128)S(1)}, u32[]{:S(2)}, u32[]{:S(2)}) collective-permute-start(f32[2,1024]{1,0:T(2,128)S(1)} %get-tuple-element.23), channel_id=1, source_target_pairs={{0,2},{2,0},{1,3},{3,1},{4,6},{6,4},{5,7},{7,5},{8,10},{10,8},{9,1... | collective-permute-start | bytes 24584 | tf_op jit(solution)/shard_map/ppermute | solution.py:24
  137.7 3.8 %collective-permute-start.23 = (f32[2,1024]{1,0:T(2,128)S(1)}, f32[2,1024]{1,0:T(2,128)S(1)}, u32[]{:S(2)}, u32[]{:S(2)}) collective-permute-start(f32[2,1024]{1,0:T(2,128)S(1)} %get-tuple-element.23), channel_id=1, source_target_pairs={{0,1},{1,0},{2,3},{3,2},{4,5},{5,4},{6,7},{7,6},{8,9},{9,8},{10,11... | collective-permute-start | bytes 24584 | tf_op jit(solution)/shard_map/ppermute | solution.py:24

commit v4 on v3

--- a/solution.py
+++ b/solution.py
@@ -10,7 +10,7 @@
 DOM = ("xl", "z", "y")
 ORB = ("xh", "c")
 
-PEERS = (1, 3, 2)
+PEERS = (2, 1, 3)
 GROUPS = (3, 2, 3)
 EARLY, LATE = GROUPS[0] + GROUPS[1], GROUPS[2]
 PAIRS = tuple((l, l) for l in range(4)) + tuple((l, l + 1) for l in range(3)) + tuple((l + 1, l) for l in range(3))
@@ -131,10 +131,7 @@
             out[0, 2 * pair + m] = mine
             wide = mine.astype(jnp.float32)
             total = total + wide * wide * occupation[pl.ds(slots[g, 2 * pair + m], 1), :]
-    summed = lax.dot_general(
-        jnp.ones((8, 128), jnp.float32), total, (((1,), (1,)), ((), ())),
-        precision=lax.Precision.HIGHEST, preferred_element_type=jnp.float32,
-    )[:1]
+    summed = jnp.sum(total.T, axis=0, keepdims=True)
     density[pl.ds(g, 1), pl.ds(pl.multiple_of(p * CHUNK, CHUNK), CHUNK)] = summed
 
 

time: 142 us -> 139 us (0.979)
  waiting for transfers between devices: 70.5 us -> 61.8 us
  starting transfers between devices: 48 us -> 53.7 us
    ppermute x26, waiting for transfers between devices: 70.5 us -> 61.8 us  [permute(): return lax.ppermute(x, axis, [(i, target(i) % size) for i in range(size)])]
    ppermute x26, starting transfers between devices: 48 us -> 53.7 us  [permute(): return lax.ppermute(x, axis, [(i, target(i) % size) for i in range(size)])]
  transfers between devices with their start and end apart: 26 -> 26, of which waited for: 15 -> 13; matrix products, arithmetic and copies ran while one was open for 1% -> 1% of each run, Pallas kernels for 4% -> 4%
where the time goes in v4:
time: 139 us
  waiting for transfers between devices  61.8 us (44%)
  starting transfers between devices  53.7 us (39%)
  Pallas kernels  12.3 us (9%)
  local copies, waits for them, and re-layouts  8.55 us (6%)
  other arithmetic  1.55 us (1%)
    ppermute x26, waiting for transfers between devices, permute(): return lax.ppermute(x, axis, [(i, target(i) % size) for i in range(size)])  61.8 us
    ppermute x26, starting transfers between devices, permute(): return lax.ppermute(x, axis, [(i, target(i) % size) for i in range(size)])  53.7 us
    unnamed x39, local copies, waits for them, and re-layouts  8.46 us
    pallas_call x1, Pallas kernels, rotate(): pl.pallas_call(rotate_kernel, grid=(blocks, points // CHUNK), out_shape=[...  7.27 us
    pallas_call x3, Pallas kernels, pack(): pl.pallas_call(pack_kernel, out_shape=[shape] * len(slots), in_specs=[SME...  3.02 us
  transfers between devices with their start and end apart: 26, of which 13 were waited for; matrix products, arithmetic and copies ran while one was open for 1% of the time, Pallas kernels for 4%

profile of v4, /device:TPU:1, one launch (start us, length us, event | category | flops | bytes accessed | tf_op | source)
XLA Modules:
  0.0 138.6 jit_solution(12958687243235988427)
XLA Ops:
  0.6 0.0 copy-start.16
  0.7 3.6 %collective-permute-start.21 = (bf16[2,4,1024,128]{3,2,1,0:T(8,128)(2,1)}, bf16[2,4,1024,128]{3,2,1,0:T(8,128)(2,1)S(1)}, u32[]{:S(2)}, u32[]{:S(2)}) collective-permute-start(bf16[2,4,1024,128]{3,2,1,0:T(8,128)(2,1)} %refs_7_.1), channel_id=1, source_target_pairs={{0,2},{2,0},{1,3},{3,1},{4,6},{6,4},{5,7},{7,5},{8,10},{10,8},{9,1... | collective-permute-start | bytes 6291464 | tf_op jit(solution)/shard_map/ppermute | solution.py:24
  4.3 1.0 collective-permute-start.20
  5.3 43.7 %collective-permute-done.21.refs_9_ = bf16[2,4,1024,128]{3,2,1,0:T(8,128)(2,1)S(1)} collective-permute-done((bf16[2,4,1024,128]{3,2,1,0:T(8,128)(2,1)}, bf16[2,4,1024,128]{3,2,1,0:T(8,128)(2,1)S(1)}, u32[]{:S(2)}, u32[]{:S(2)}) %collective-permute-start.21) | collective-permute-done | bytes 2097184 | tf_op jit(solution)/shard_map/ppermute | solution.py:24
  48.9 2.2 %collective-permute-start.22 = (bf16[2,4,1024,128]{3,2,1,0:T(8,128)(2,1)S(1)}, bf16[2,4,1024,128]{3,2,1,0:T(8,128)(2,1)}, u32[]{:S(2)}, u32[]{:S(2)}) collective-permute-start(bf16[2,4,1024,128]{3,2,1,0:T(8,128)(2,1)S(1)} %collective-permute-done.21.refs_9_), channel_id=1, source_target_pairs={{0,1},{1,0},{2,3},{3,2},{4,5},{5,4},{6,7},{7,6},{8,9},{9,8},{10,11... | collective-permute-start | bytes 6291464 | tf_op jit(solution)/shard_map/ppermute | solution.py:24
  51.1 1.4 %collective-permute-start = (bf16[48,8,128]{2,1,0:T(8,128)(2,1)}, bf16[48,8,128]{2,1,0:T(8,128)(2,1)S(1)}, u32[]{:S(2)}, u32[]{:S(2)}) collective-permute-start(bf16[48,8,128]{2,1,0:T(8,128)(2,1)} %bitcast.14), channel_id=1, source_target_pairs={{0,128},{128,0},{1,129},{129,1},{2,130},{130,2},{3,131},{131,3},{4... | collective-permute-start | bytes 294920 | tf_op jit(solution)/shard_map/ppermute | solution.py:24
  52.5 3.1 %collective-permute-done = bf16[48,8,128]{2,1,0:T(8,128)(2,1)S(1)} collective-permute-done((bf16[48,8,128]{2,1,0:T(8,128)(2,1)}, bf16[48,8,128]{2,1,0:T(8,128)(2,1)S(1)}, u32[]{:S(2)}, u32[]{:S(2)}) %collective-permute-start) | collective-permute-done | bytes 98336 | tf_op jit(solution)/shard_map/ppermute | solution.py:24
  55.7 0.9 pad_maximum_fusion.refs_3_.refs_0_
  56.6 6.3 %collective-permute-start.4 = (bf16[2,48,8,128]{3,2,1,0:T(8,128)(2,1)S(1)}, bf16[2,48,8,128]{3,2,1,0:T(8,128)(2,1)S(1)}, u32[]{:S(2)}, u32[]{:S(2)}) collective-permute-start(bf16[2,48,8,128]{3,2,1,0:T(8,128)(2,1)S(1)} %pad_maximum_fusion.refs_3_.refs_0_), channel_id=1, source_target_pairs={{0,96},{16,112},{32,64},{48,80},{64,32},{80,48},{96,0},{112,16},{1... | collective-permute-start | bytes 589832 | tf_op jit(solution)/shard_map/ppermute | solution.py:24
  62.9 2.7 %collective-permute-start.7 = (s32[2,4]{1,0:T(2,128)}, s32[2,4]{1,0:T(2,128)S(1)}, u32[]{:S(2)}, u32[]{:S(2)}) collective-permute-start(s32[2,4]{1,0:T(2,128)} %slots.3), channel_id=1, source_target_pairs={{0,12},{4,8},{8,4},{12,0},{1,13},{5,9},{9,5},{13,1},{2,14},{6,10},... | collective-permute-start | bytes 104 | tf_op jit(solution)/shard_map/ppermute | solution.py:24
  65.6 1.2 collective-permute-start.3
  66.8 0.3 collective-permute-done.7.refs_2_
  67.1 0.0 collective-permute-start.6
  67.1 2.6 %collective-permute-done.6.refs_1_ = s32[2,4]{1,0:T(2,128)S(1)} collective-permute-done((s32[2,4]{1,0:T(2,128)}, s32[2,4]{1,0:T(2,128)S(1)}, u32[]{:S(2)}, u32[]{:S(2)}) %collective-permute-start.6) | collective-permute-done | bytes 64 | tf_op jit(solution)/shard_map/ppermute | solution.py:24
  69.7 2.7 %collective-permute-start.5 = (s32[2,4]{1,0:T(2,128)}, s32[2,4]{1,0:T(2,128)S(1)}, u32[]{:S(2)}, u32[]{:S(2)}) collective-permute-start(s32[2,4]{1,0:T(2,128)} %slots.3), channel_id=1, source_target_pairs={{0,8},{4,12},{8,0},{12,4},{1,9},{5,13},{9,1},{13,5},{2,10},{6,14},... | collective-permute-start | bytes 104 | tf_op jit(solution)/shard_map/ppermute | solution.py:24
  72.4 1.5 %collective-permute-done.5.refs_0_ = s32[2,4]{1,0:T(2,128)S(1)} collective-permute-done((s32[2,4]{1,0:T(2,128)}, s32[2,4]{1,0:T(2,128)S(1)}, u32[]{:S(2)}, u32[]{:S(2)}) %collective-permute-start.5) | collective-permute-done | bytes 64 | tf_op jit(solution)/shard_map/ppermute | solution.py:24
  73.9 0.0 collective-permute-start.2
  73.9 0.0 collective-permute-done.4.refs_4_
  73.9 1.5 %collective-permute-start.1 = (bf16[2,48,8,128]{3,2,1,0:T(8,128)(2,1)S(1)}, bf16[2,48,8,128]{3,2,1,0:T(8,128)(2,1)S(1)}, u32[]{:S(2)}, u32[]{:S(2)}) collective-permute-start(bf16[2,48,8,128]{3,2,1,0:T(8,128)(2,1)S(1)} %pad_maximum_fusion.refs_3_.refs_0_), channel_id=1, source_target_pairs={{0,16},{16,0},{32,48},{48,32},{64,80},{80,64},{96,112},{112,96},{1... | collective-permute-start | bytes 589832 | tf_op jit(solution)/shard_map/ppermute | solution.py:24
  75.4 0.7 shard_map.78
  76.1 3.0 %collective-permute-start.11 = (bf16[20,2,2,8,128]{4,3,2,1,0:T(8,128)(2,1)S(1)}, bf16[20,2,2,8,128]{4,3,2,1,0:T(8,128)(2,1)S(1)}, u32[]{:S(2)}, u32[]{:S(2)}) collective-permute-start(bf16[20,2,2,8,128]{4,3,2,1,0:T(8,128)(2,1)S(1)} %get-tuple-element.16), channel_id=1, source_target_pairs={{0,8},{4,12},{8,0},{12,4},{1,9},{5,13},{9,1},{13,5},{2,10},{6,14},... | collective-permute-start | bytes 491528 | tf_op jit(solution)/shard_map/ppermute | solution.py:24
  79.1 0.5 collective-permute-done.2.refs_5_.refs_2_
  79.6 0.9 collective-permute-start.12
  80.5 2.4 %collective-permute-start.13 = (bf16[20,2,2,8,128]{4,3,2,1,0:T(8,128)(2,1)S(1)}, bf16[20,2,2,8,128]{4,3,2,1,0:T(8,128)(2,1)S(1)}, u32[]{:S(2)}, u32[]{:S(2)}) collective-permute-start(bf16[20,2,2,8,128]{4,3,2,1,0:T(8,128)(2,1)S(1)} %get-tuple-element.18), channel_id=1, source_target_pairs={{0,12},{4,8},{8,4},{12,0},{1,13},{5,9},{9,5},{13,1},{2,14},{6,10},... | collective-permute-start | bytes 491528 | tf_op jit(solution)/shard_map/ppermute | solution.py:24
  82.9 0.0 collective-permute-done.11.refs_8_
  82.9 1.7 %collective-permute-start.16 = (bf16[2,48,8,128]{3,2,1,0:T(8,128)(2,1)S(1)}, bf16[2,48,8,128]{3,2,1,0:T(8,128)(2,1)S(1)}, u32[]{:S(2)}, u32[]{:S(2)}) collective-permute-start(bf16[2,48,8,128]{3,2,1,0:T(8,128)(2,1)S(1)} %collective-permute-done.4.refs_4_), channel_id=1, source_target_pairs={{0,32},{16,48},{32,0},{48,16},{64,96},{80,112},{96,64},{112,80},{1... | collective-permute-start | bytes 589832 | tf_op jit(solution)/shard_map/ppermute | solution.py:24
  84.6 1.0 collective-permute-start.15
  85.7 1.1 collective-permute-done.13.refs_10_
  86.7 0.1 collective-permute-start.14
  86.9 0.7 shard_map.77
  87.6 3.3 %collective-permute-done.16.refs_5_.refs_2_ = bf16[2,48,8,128]{3,2,1,0:T(8,128)(2,1)S(1)} collective-permute-done((bf16[2,48,8,128]{3,2,1,0:T(8,128)(2,1)S(1)}, bf16[2,48,8,128]{3,2,1,0:T(8,128)(2,1)S(1)}, u32[]{:S(2)}, u32[]{:S(2)}) %collective-permute-start.16) | collective-permute-done | bytes 196640 | tf_op jit(solution)/shard_map/ppermute | solution.py:24
  90.9 1.2 collective-permute-start.8
  92.0 0.0 collective-permute-done.15.refs_4_.refs_1_
  92.0 0.9 collective-permute-start.9
  92.9 0.0 collective-permute-done.14.refs_3_.refs_0_
  92.9 2.2 %collective-permute-start.10 = (bf16[20,3,2,8,128]{4,3,2,1,0:T(8,128)(2,1)S(1)}, bf16[20,3,2,8,128]{4,3,2,1,0:T(8,128)(2,1)S(1)}, u32[]{:S(2)}, u32[]{:S(2)}) collective-permute-start(bf16[20,3,2,8,128]{4,3,2,1,0:T(8,128)(2,1)S(1)} %get-tuple-element.15), channel_id=1, source_target_pairs={{0,12},{4,8},{8,4},{12,0},{1,13},{5,9},{9,5},{13,1},{2,14},{6,10},... | collective-permute-start | bytes 737288 | tf_op jit(solution)/shard_map/ppermute | solution.py:24
  95.1 1.6 %shard_map.80 = (bf16[20,3,2,8,128]{4,3,2,1,0:T(8,128)(2,1)}, bf16[20,3,2,8,128]{4,3,2,1,0:T(8,128)(2,1)}, bf16[20,3,2,8,128]{4,3,2,1,0:T(8,128)(2,1)}) custom-call(s32[2,4]{1,0:T(2,128)S(1)} %collective-permute-done.5.refs_0_, s32[2,4]{1,0:T(2,128)S(1)} %collective-permute-done.6.refs_1_, s32[2,4]{1,0:T(2,128)S(1)} %collective-permute-done.7.refs_2_, ...), custom_call_target="tpu_custom_call" | custom-call | flops 1000000 | bytes 2000000 | tf_op jit(solution)/shard_map/pallas_call | solution.py:45
  96.7 0.7 copy-done.1
  97.4 0.1 collective-permute-done.8.refs_5_
  97.5 0.7 copy-done.3
  98.2 1.4 %collective-permute-start.17 = (bf16[20,3,2,8,128]{4,3,2,1,0:T(8,128)(2,1)}, bf16[20,3,2,8,128]{4,3,2,1,0:T(8,128)(2,1)}, u32[]{:S(2)}, u32[]{:S(2)}) collective-permute-start(bf16[20,3,2,8,128]{4,3,2,1,0:T(8,128)(2,1)} %get-tuple-element.19), channel_id=1, source_target_pairs={{0,8},{4,12},{8,0},{12,4},{1,9},{5,13},{9,1},{13,5},{2,10},{6,14},... | collective-permute-start | bytes 737288 | tf_op jit(solution)/shard_map/ppermute | solution.py:24
  99.6 0.7 copy-done.5
  100.3 0.6 collective-permute-start.18
  100.9 0.7 copy-done.7
  101.6 1.3 collective-permute-start.19
  102.9 0.1 copy.9.pattern
  103.0 0.1 stack.53.meta
  103.1 0.0 copy-start.4
  103.1 0.9 copy-done.4
  104.0 0.9 copy-done.6
  105.0 0.9 copy-done.8
  105.9 0.9 copy-done.10
  106.8 0.9 copy-done.12
  107.7 0.9 copy-done.14
  108.7 2.0 %shard_map.79.staged = bf16[2,2,1536,256]{3,2,1,0:T(8,128)(2,1)S(1)} custom-call(s32[11]{0:T(128)S(1)} %stack.53.meta, s32[2,4]{1,0:T(2,128)S(1)} %copy-done.16, s32[2]{0:T(128)S(1)} %copy-done.17, s32[16,3]{1,0:T(8,128)S(1)} %copy.9.pattern, bf16[2,48,8,128]{3,2,1,0:T(8,128)(2,1)S(1)} %pad_maximum_fusion.refs_3_.refs_0_, ...), custom_call_target="tpu_custom_call" | custom-call | flops 1000000 | bytes 6000000 | tf_op jit(solution)/shard_map/pallas_call | solution.py:100
  110.7 1.3 collective-permute-done.18.refs_4_
  112.0 0.8 collective-permute-done.19.refs_5_
  112.8 7.3 %shard_map.81 = (bf16[2,4,1024,128]{3,2,1,0:T(8,128)(2,1)}, f32[2,1024]{1,0:T(2,128)S(1)}) custom-call(s32[11]{0:T(128)S(1)} %stack.53.meta, s32[2,4]{1,0:T(2,128)S(1)} %copy-done.16, s32[2]{0:T(128)S(1)} %copy-done.17, s32[16,3]{1,0:T(8,128)S(1)} %copy.9.pattern, bf16[2,2,1536,256]{3,2,1,0:T(8,128)(2,1)S(1)} %shard_map.79.staged, ...), custom_call_target="tpu_custom_call" | custom-call | flops 3000000000 | bytes 14000000 | tf_op jit(solution)/shard_map/pallas_call | solution.py:141
  120.1 13.9 %collective-permute-start.25 = (f32[2,1024]{1,0:T(2,128)S(1)}, f32[2,1024]{1,0:T(2,128)S(1)}, u32[]{:S(2)}, u32[]{:S(2)}) collective-permute-start(f32[2,1024]{1,0:T(2,128)S(1)} %get-tuple-element.23), channel_id=1, source_target_pairs={{0,3},{1,2},{2,1},{3,0},{4,7},{5,6},{6,5},{7,4},{8,11},{9,10},{10,... | collective-permute-start | bytes 24584 | tf_op jit(solution)/shard_map/ppermute | solution.py:24
  134.0 0.2 collective-permute-start.24
  134.2 0.3 collective-permute-start.23
  134.5 1.1 collective-permute-done.25
  135.5 2.4 %collective-permute-done.24 = f32[2,1024]{1,0:T(2,128)S(1)} collective-permute-done((f32[2,1024]{1,0:T(2,128)S(1)}, f32[2,1024]{1,0:T(2,128)S(1)}, u32[]{:S(2)}, u32[]{:S(2)}) %collective-permute-start.24) | collective-permute-done | bytes 8224 | tf_op jit(solution)/shard_map/ppermute | solution.py:24
  138.0 0.6 add_add_fusion
  (36 shorter events, 0.1 us)
Async XLA Ops:
  0.6 102.4 %copy-start.16 = (s32[2,4]{1,0:T(2,128)S(1)}, s32[2,4]{1,0:T(2,128)}, u32[]{:S(2)}) copy-start(s32[2,4]{1,0:T(2,128)} %slots.3) | copy-start | bytes 100
  0.6 102.2 %copy-start.18 = (s32[16,3]{0,1:T(4,128)S(1)}, s32[16,3]{0,1:T(4,128)}, u32[]{:S(2)}) copy-start(s32[16,3]{0,1:T(4,128)} %param.10) | copy-start | bytes 580
  0.7 102.4 %copy-start.17 = (s32[2]{0:T(128)S(1)}, s32[2]{0:T(128)}, u32[]{:S(2)}) copy-start(s32[2]{0:T(128)} %counts.3) | copy-start | bytes 28
  0.7 48.3 %collective-permute-start.21 = (bf16[2,4,1024,128]{3,2,1,0:T(8,128)(2,1)}, bf16[2,4,1024,128]{3,2,1,0:T(8,128)(2,1)S(1)}, u32[]{:S(2)}, u32[]{:S(2)}) collective-permute-start(bf16[2,4,1024,128]{3,2,1,0:T(8,128)(2,1)} %refs_7_.1), channel_id=1, source_target_pairs={{0,2},{2,0},{1,3},{3,1},{4,6},{6,4},{5,7},{7,5},{8,10},{10,8},{9,1... | collective-permute-start | bytes 6291464 | tf_op jit(solution)/shard_map/ppermute | solution.py:24
  4.3 108.5 %collective-permute-start.20 = (bf16[2,4,1024,128]{3,2,1,0:T(8,128)(2,1)}, bf16[2,4,1024,128]{3,2,1,0:T(8,128)(2,1)}, u32[]{:S(2)}, u32[]{:S(2)}) collective-permute-start(bf16[2,4,1024,128]{3,2,1,0:T(8,128)(2,1)} %refs_7_.1), channel_id=1, source_target_pairs={{0,1},{1,0},{2,3},{3,2},{4,5},{5,4},{6,7},{7,6},{8,9},{9,8},{10,11... | collective-permute-start | bytes 6291464 | tf_op jit(solution)/shard_map/ppermute | solution.py:24
  48.9 63.8 %collective-permute-start.22 = (bf16[2,4,1024,128]{3,2,1,0:T(8,128)(2,1)S(1)}, bf16[2,4,1024,128]{3,2,1,0:T(8,128)(2,1)}, u32[]{:S(2)}, u32[]{:S(2)}) collective-permute-start(bf16[2,4,1024,128]{3,2,1,0:T(8,128)(2,1)S(1)} %collective-permute-done.21.refs_9_), channel_id=1, source_target_pairs={{0,1},{1,0},{2,3},{3,2},{4,5},{5,4},{6,7},{7,6},{8,9},{9,8},{10,11... | collective-permute-start | bytes 6291464 | tf_op jit(solution)/shard_map/ppermute | solution.py:24
  51.1 4.6 %collective-permute-start = (bf16[48,8,128]{2,1,0:T(8,128)(2,1)}, bf16[48,8,128]{2,1,0:T(8,128)(2,1)S(1)}, u32[]{:S(2)}, u32[]{:S(2)}) collective-permute-start(bf16[48,8,128]{2,1,0:T(8,128)(2,1)} %bitcast.14), channel_id=1, source_target_pairs={{0,128},{128,0},{1,129},{129,1},{2,130},{130,2},{3,131},{131,3},{4... | collective-permute-start | bytes 294920 | tf_op jit(solution)/shard_map/ppermute | solution.py:24
  56.6 17.3 %collective-permute-start.4 = (bf16[2,48,8,128]{3,2,1,0:T(8,128)(2,1)S(1)}, bf16[2,48,8,128]{3,2,1,0:T(8,128)(2,1)S(1)}, u32[]{:S(2)}, u32[]{:S(2)}) collective-permute-start(bf16[2,48,8,128]{3,2,1,0:T(8,128)(2,1)S(1)} %pad_maximum_fusion.refs_3_.refs_0_), channel_id=1, source_target_pairs={{0,96},{16,112},{32,64},{48,80},{64,32},{80,48},{96,0},{112,16},{1... | collective-permute-start | bytes 589832 | tf_op jit(solution)/shard_map/ppermute | solution.py:24
  62.9 4.2 %collective-permute-start.7 = (s32[2,4]{1,0:T(2,128)}, s32[2,4]{1,0:T(2,128)S(1)}, u32[]{:S(2)}, u32[]{:S(2)}) collective-permute-start(s32[2,4]{1,0:T(2,128)} %slots.3), channel_id=1, source_target_pairs={{0,12},{4,8},{8,4},{12,0},{1,13},{5,9},{9,5},{13,1},{2,14},{6,10},... | collective-permute-start | bytes 104 | tf_op jit(solution)/shard_map/ppermute | solution.py:24
  65.6 9.7 %collective-permute-start.3 = (bf16[2,48,8,128]{3,2,1,0:T(8,128)(2,1)S(1)}, bf16[2,48,8,128]{3,2,1,0:T(8,128)(2,1)S(1)}, u32[]{:S(2)}, u32[]{:S(2)}) collective-permute-start(bf16[2,48,8,128]{3,2,1,0:T(8,128)(2,1)S(1)} %pad_maximum_fusion.refs_3_.refs_0_), channel_id=1, source_target_pairs={{0,32},{16,48},{32,0},{48,16},{64,96},{80,112},{96,64},{112,80},{1... | collective-permute-start | bytes 589832 | tf_op jit(solution)/shard_map/ppermute | solution.py:24
  67.1 2.6 %collective-permute-start.6 = (s32[2,4]{1,0:T(2,128)}, s32[2,4]{1,0:T(2,128)S(1)}, u32[]{:S(2)}, u32[]{:S(2)}) collective-permute-start(s32[2,4]{1,0:T(2,128)} %slots.3), channel_id=1, source_target_pairs={{0,4},{4,0},{8,12},{12,8},{1,5},{5,1},{9,13},{13,9},{2,6},{6,2},{1... | collective-permute-start | bytes 104 | tf_op jit(solution)/shard_map/ppermute | solution.py:24
  69.7 4.1 %collective-permute-start.5 = (s32[2,4]{1,0:T(2,128)}, s32[2,4]{1,0:T(2,128)S(1)}, u32[]{:S(2)}, u32[]{:S(2)}) collective-permute-start(s32[2,4]{1,0:T(2,128)} %slots.3), channel_id=1, source_target_pairs={{0,8},{4,12},{8,0},{12,4},{1,9},{5,13},{9,1},{13,5},{2,10},{6,14},... | collective-permute-start | bytes 104 | tf_op jit(solution)/shard_map/ppermute | solution.py:24
  73.9 5.7 %collective-permute-start.2 = (bf16[2,48,8,128]{3,2,1,0:T(8,128)(2,1)S(1)}, bf16[2,48,8,128]{3,2,1,0:T(8,128)(2,1)S(1)}, u32[]{:S(2)}, u32[]{:S(2)}) collective-permute-start(bf16[2,48,8,128]{3,2,1,0:T(8,128)(2,1)S(1)} %pad_maximum_fusion.refs_3_.refs_0_), channel_id=1, source_target_pairs={{0,112},{16,32},{32,16},{48,64},{64,48},{80,96},{96,80},{112,0},{1... | collective-permute-start | bytes 589832 | tf_op jit(solution)/shard_map/ppermute | solution.py:24
  73.9 6.6 %collective-permute-start.1 = (bf16[2,48,8,128]{3,2,1,0:T(8,128)(2,1)S(1)}, bf16[2,48,8,128]{3,2,1,0:T(8,128)(2,1)S(1)}, u32[]{:S(2)}, u32[]{:S(2)}) collective-permute-start(bf16[2,48,8,128]{3,2,1,0:T(8,128)(2,1)S(1)} %pad_maximum_fusion.refs_3_.refs_0_), channel_id=1, source_target_pairs={{0,16},{16,0},{32,48},{48,32},{64,80},{80,64},{96,112},{112,96},{1... | collective-permute-start | bytes 589832 | tf_op jit(solution)/shard_map/ppermute | solution.py:24
  76.1 6.9 %collective-permute-start.11 = (bf16[20,2,2,8,128]{4,3,2,1,0:T(8,128)(2,1)S(1)}, bf16[20,2,2,8,128]{4,3,2,1,0:T(8,128)(2,1)S(1)}, u32[]{:S(2)}, u32[]{:S(2)}) collective-permute-start(bf16[20,2,2,8,128]{4,3,2,1,0:T(8,128)(2,1)S(1)} %get-tuple-element.16), channel_id=1, source_target_pairs={{0,8},{4,12},{8,0},{12,4},{1,9},{5,13},{9,1},{13,5},{2,10},{6,14},... | collective-permute-start | bytes 491528 | tf_op jit(solution)/shard_map/ppermute | solution.py:24
  79.6 5.0 %collective-permute-start.12 = (bf16[20,2,2,8,128]{4,3,2,1,0:T(8,128)(2,1)S(1)}, bf16[20,2,2,8,128]{4,3,2,1,0:T(8,128)(2,1)S(1)}, u32[]{:S(2)}, u32[]{:S(2)}) collective-permute-start(bf16[20,2,2,8,128]{4,3,2,1,0:T(8,128)(2,1)S(1)} %get-tuple-element.17), channel_id=1, source_target_pairs={{0,4},{4,0},{8,12},{12,8},{1,5},{5,1},{9,13},{13,9},{2,6},{6,2},{1... | collective-permute-start | bytes 491528 | tf_op jit(solution)/shard_map/ppermute | solution.py:24
  80.5 6.3 %collective-permute-start.13 = (bf16[20,2,2,8,128]{4,3,2,1,0:T(8,128)(2,1)S(1)}, bf16[20,2,2,8,128]{4,3,2,1,0:T(8,128)(2,1)S(1)}, u32[]{:S(2)}, u32[]{:S(2)}) collective-permute-start(bf16[20,2,2,8,128]{4,3,2,1,0:T(8,128)(2,1)S(1)} %get-tuple-element.18), channel_id=1, source_target_pairs={{0,12},{4,8},{8,4},{12,0},{1,13},{5,9},{9,5},{13,1},{2,14},{6,10},... | collective-permute-start | bytes 491528 | tf_op jit(solution)/shard_map/ppermute | solution.py:24
  82.9 17.9 %copy-start.9 = (bf16[20,2,2,8,128]{4,3,2,1,0:T(8,128)(2,1)}, bf16[20,2,2,8,128]{4,3,2,1,0:T(8,128)(2,1)S(1)}, u32[]{:S(2)}) copy-start(bf16[20,2,2,8,128]{4,3,2,1,0:T(8,128)(2,1)S(1)} %collective-permute-done.11.refs_8_) | copy-start | bytes 491524
  82.9 7.9 %collective-permute-start.16 = (bf16[2,48,8,128]{3,2,1,0:T(8,128)(2,1)S(1)}, bf16[2,48,8,128]{3,2,1,0:T(8,128)(2,1)S(1)}, u32[]{:S(2)}, u32[]{:S(2)}) collective-permute-start(bf16[2,48,8,128]{3,2,1,0:T(8,128)(2,1)S(1)} %collective-permute-done.4.refs_4_), channel_id=1, source_target_pairs={{0,32},{16,48},{32,0},{48,16},{64,96},{80,112},{96,64},{112,80},{1... | collective-permute-start | bytes 589832 | tf_op jit(solution)/shard_map/ppermute | solution.py:24
  84.6 17.0 %copy-start.11 = (bf16[20,2,2,8,128]{4,3,2,1,0:T(8,128)(2,1)}, bf16[20,2,2,8,128]{4,3,2,1,0:T(8,128)(2,1)S(1)}, u32[]{:S(2)}) copy-start(bf16[20,2,2,8,128]{4,3,2,1,0:T(8,128)(2,1)S(1)} %collective-permute-done.12.refs_9_) | copy-start | bytes 491524
  84.6 7.4 %collective-permute-start.15 = (bf16[2,48,8,128]{3,2,1,0:T(8,128)(2,1)S(1)}, bf16[2,48,8,128]{3,2,1,0:T(8,128)(2,1)S(1)}, u32[]{:S(2)}, u32[]{:S(2)}) collective-permute-start(bf16[2,48,8,128]{3,2,1,0:T(8,128)(2,1)S(1)} %get-tuple-element.24), channel_id=1, source_target_pairs={{0,112},{16,32},{32,16},{48,64},{64,48},{80,96},{96,80},{112,0},{1... | collective-permute-start | bytes 589832 | tf_op jit(solution)/shard_map/ppermute | solution.py:24
  86.7 14.8 %copy-start.13 = (bf16[20,2,2,8,128]{4,3,2,1,0:T(8,128)(2,1)}, bf16[20,2,2,8,128]{4,3,2,1,0:T(8,128)(2,1)S(1)}, u32[]{:S(2)}) copy-start(bf16[20,2,2,8,128]{4,3,2,1,0:T(8,128)(2,1)S(1)} %collective-permute-done.13.refs_10_) | copy-start | bytes 491524
  86.7 6.2 %collective-permute-start.14 = (bf16[2,48,8,128]{3,2,1,0:T(8,128)(2,1)S(1)}, bf16[2,48,8,128]{3,2,1,0:T(8,128)(2,1)S(1)}, u32[]{:S(2)}, u32[]{:S(2)}) collective-permute-start(bf16[2,48,8,128]{3,2,1,0:T(8,128)(2,1)S(1)} %get-tuple-element.25), channel_id=1, source_target_pairs={{0,16},{16,0},{32,48},{48,32},{64,80},{80,64},{96,112},{112,96},{1... | collective-permute-start | bytes 589832 | tf_op jit(solution)/shard_map/ppermute | solution.py:24
  90.9 6.6 %collective-permute-start.8 = (bf16[20,3,2,8,128]{4,3,2,1,0:T(8,128)(2,1)S(1)}, bf16[20,3,2,8,128]{4,3,2,1,0:T(8,128)(2,1)S(1)}, u32[]{:S(2)}, u32[]{:S(2)}) collective-permute-start(bf16[20,3,2,8,128]{4,3,2,1,0:T(8,128)(2,1)S(1)} %get-tuple-element.13), channel_id=1, source_target_pairs={{0,8},{4,12},{8,0},{12,4},{1,9},{5,13},{9,1},{13,5},{2,10},{6,14},... | collective-permute-start | bytes 737288 | tf_op jit(solution)/shard_map/ppermute | solution.py:24
  92.0 7.5 %collective-permute-start.9 = (bf16[20,3,2,8,128]{4,3,2,1,0:T(8,128)(2,1)S(1)}, bf16[20,3,2,8,128]{4,3,2,1,0:T(8,128)(2,1)S(1)}, u32[]{:S(2)}, u32[]{:S(2)}) collective-permute-start(bf16[20,3,2,8,128]{4,3,2,1,0:T(8,128)(2,1)S(1)} %get-tuple-element.14), channel_id=1, source_target_pairs={{0,4},{4,0},{8,12},{12,8},{1,5},{5,1},{9,13},{13,9},{2,6},{6,2},{1... | collective-permute-start | bytes 737288 | tf_op jit(solution)/shard_map/ppermute | solution.py:24
  92.9 8.0 %collective-permute-start.10 = (bf16[20,3,2,8,128]{4,3,2,1,0:T(8,128)(2,1)S(1)}, bf16[20,3,2,8,128]{4,3,2,1,0:T(8,128)(2,1)S(1)}, u32[]{:S(2)}, u32[]{:S(2)}) collective-permute-start(bf16[20,3,2,8,128]{4,3,2,1,0:T(8,128)(2,1)S(1)} %get-tuple-element.15), channel_id=1, source_target_pairs={{0,12},{4,8},{8,4},{12,0},{1,13},{5,9},{9,5},{13,1},{2,14},{6,10},... | collective-permute-start | bytes 737288 | tf_op jit(solution)/shard_map/ppermute | solution.py:24
  96.7 0.7 copy-start.1
  97.5 0.7 copy-start.3
  98.2 12.5 %collective-permute-start.17 = (bf16[20,3,2,8,128]{4,3,2,1,0:T(8,128)(2,1)}, bf16[20,3,2,8,128]{4,3,2,1,0:T(8,128)(2,1)}, u32[]{:S(2)}, u32[]{:S(2)}) collective-permute-start(bf16[20,3,2,8,128]{4,3,2,1,0:T(8,128)(2,1)} %get-tuple-element.19), channel_id=1, source_target_pairs={{0,8},{4,12},{8,0},{12,4},{1,9},{5,13},{9,1},{13,5},{2,10},{6,14},... | collective-permute-start | bytes 737288 | tf_op jit(solution)/shard_map/ppermute | solution.py:24
  99.6 0.7 copy-start.5
  100.3 11.7 %collective-permute-start.18 = (bf16[20,3,2,8,128]{4,3,2,1,0:T(8,128)(2,1)}, bf16[20,3,2,8,128]{4,3,2,1,0:T(8,128)(2,1)}, u32[]{:S(2)}, u32[]{:S(2)}) collective-permute-start(bf16[20,3,2,8,128]{4,3,2,1,0:T(8,128)(2,1)} %get-tuple-element.20), channel_id=1, source_target_pairs={{0,4},{4,0},{8,12},{12,8},{1,5},{5,1},{9,13},{13,9},{2,6},{6,2},{1... | collective-permute-start | bytes 737288 | tf_op jit(solution)/shard_map/ppermute | solution.py:24
  100.9 0.7 copy-start.7
  101.6 11.2 %collective-permute-start.19 = (bf16[20,3,2,8,128]{4,3,2,1,0:T(8,128)(2,1)}, bf16[20,3,2,8,128]{4,3,2,1,0:T(8,128)(2,1)}, u32[]{:S(2)}, u32[]{:S(2)}) collective-permute-start(bf16[20,3,2,8,128]{4,3,2,1,0:T(8,128)(2,1)} %get-tuple-element.21), channel_id=1, source_target_pairs={{0,12},{4,8},{8,4},{12,0},{1,13},{5,9},{9,5},{13,1},{2,14},{6,10},... | collective-permute-start | bytes 737288 | tf_op jit(solution)/shard_map/ppermute | solution.py:24
  103.1 0.9 copy-start.4
  104.0 0.9 copy-start.6
  105.0 0.9 copy-start.8
  105.9 0.9 copy-start.10
  106.8 0.9 copy-start.12
  107.7 0.9 copy-start.14
  108.6 4.1 %copy-start = (bf16[2,4,1024,128]{3,2,1,0:T(8,128)(2,1)S(1)}, bf16[2,4,1024,128]{3,2,1,0:T(8,128)(2,1)}, u32[]{:S(2)}) copy-start(bf16[2,4,1024,128]{3,2,1,0:T(8,128)(2,1)} %refs_7_.1) | copy-start | bytes 6291460
  108.6 4.1 %copy-start.2 = (bf16[2,48,8,128]{3,2,1,0:T(8,128)(2,1)S(1)}, bf16[2,48,8,128]{3,2,1,0:T(8,128)(2,1)}, u32[]{:S(2)}) copy-start(bf16[2,48,8,128]{3,2,1,0:T(8,128)(2,1)} %copy-done.1) | copy-start | bytes 589828
  108.7 4.2 %copy-start.15 = (f32[16,128]{1,0:T(8,128)S(1)}, f32[16,128]{1,0:T(8,128)}, u32[]{:S(2)}) copy-start(f32[16,128]{1,0:T(8,128)} %refs_6_.1) | copy-start | bytes 24580
  120.1 15.5 %collective-permute-start.25 = (f32[2,1024]{1,0:T(2,128)S(1)}, f32[2,1024]{1,0:T(2,128)S(1)}, u32[]{:S(2)}, u32[]{:S(2)}) collective-permute-start(f32[2,1024]{1,0:T(2,128)S(1)} %get-tuple-element.23), channel_id=1, source_target_pairs={{0,3},{1,2},{2,1},{3,0},{4,7},{5,6},{6,5},{7,4},{8,11},{9,10},{10,... | collective-permute-start | bytes 24584 | tf_op jit(solution)/shard_map/ppermute | solution.py:24
  134.0 4.0 %collective-permute-start.24 = (f32[2,1024]{1,0:T(2,128)S(1)}, f32[2,1024]{1,0:T(2,128)S(1)}, u32[]{:S(2)}, u32[]{:S(2)}) collective-permute-start(f32[2,1024]{1,0:T(2,128)S(1)} %get-tuple-element.23), channel_id=1, source_target_pairs={{0,2},{2,0},{1,3},{3,1},{4,6},{6,4},{5,7},{7,5},{8,10},{10,8},{9,1... | collective-permute-start | bytes 24584 | tf_op jit(solution)/shard_map/ppermute | solution.py:24
  134.2 3.8 %collective-permute-start.23 = (f32[2,1024]{1,0:T(2,128)S(1)}, f32[2,1024]{1,0:T(2,128)S(1)}, u32[]{:S(2)}, u32[]{:S(2)}) collective-permute-start(f32[2,1024]{1,0:T(2,128)S(1)} %get-tuple-element.23), channel_id=1, source_target_pairs={{0,1},{1,0},{2,3},{3,2},{4,5},{5,4},{6,7},{7,6},{8,9},{9,8},{10,11... | collective-permute-start | bytes 24584 | tf_op jit(solution)/shard_map/ppermute | solution.py:24
